TPU v7x, 32 devices: a whole 2x2x4 slice. The times are simulated.
32 devices in a mesh: dom: 8 (over z, y), sub: 4 (over x, core).
Axes of the slice: x: 2, y: 2, z: 4, core: 2. Of those that a mesh axis runs over, the one named last changes fastest.
Arguments:
- nodal_values: float32 [512, 8192], P(None, ('dom', 'sub')), may hold values from -6 to 6
- kappa: float32 [512, 8192], P(None, ('dom', 'sub')), may hold values from 0.25 to 4
- levels: int32 [8192], P(('dom', 'sub')), may hold values from 0 to 3
- local_faces: int32 [2, 2048], P(None, ('dom', 'sub')), may hold values from 0 to 511, as said below
- sub_faces: int32 [2, 1024], P(None, ('dom', 'sub')), may hold values from 0 to 511, as said below
- near_faces: int32 [2, 1024], P(None, ('dom', 'sub')), may hold values from 512 to 1023, as said below
- far_faces: int32 [2, 384], P(None, ('dom', 'sub')), may hold values from 1024 to 1535, as said below
- child_faces: int32 [4, 96], P(None, ('dom', 'sub')), may hold values from 1024 to 1279, as said below
- child_peer: int32 [96], P(('dom', 'sub')), may hold values from 0 to 7, as said below
- coarse_faces: int32 [256], P(('dom', 'sub')), may hold values from -1 to 1535, as said below
Outputs:
- applied: float32 [512, 8192], P(None, ('dom', 'sub'))
Inputs may be any that keep to these rules, and one draw needn't show every extreme that they name: `local_faces`: row 0 holds faces f = 1 and row 1 faces f = 0 of distinct elements of the same device; column k of both rows is one shared face. `sub_faces`: row 0 holds faces f = 0, row 1 faces f = 1, of distinct elements; entries toward a missing neighbour are boundary faces. `near_faces`: row 0 holds faces f = 2, row 1 faces f = 3, of distinct elements; entries toward a missing neighbour are boundary faces. `far_faces`: row 0 holds faces f = 4, row 1 faces f = 5, of distinct elements; entries toward a missing partner are boundary faces. `child_faces`: faces f = 4 of distinct elements, distinct from all far faces; row m is the child at subface position (m // 2, m % 2). `child_peer`: A device's 3 groups name distinct dom indices other than its own; in every draw one device per sub index is named by every other dom index. `coarse_faces`: slot p is the face f = 5 that takes the group which the device of dom index p (same sub index) sends here, -1 where it sends none; faces are of distinct elements, distinct from all far faces.
All inputs are finite; a program needn't handle non-finite values.
Results may differ from a plain program's by a relative error of at most 0.0003.
Values sent between devices are 32-bit elements; how exact they have to be, the bound alone decides.
A program may use at most 64 MiB of HBM per device.

v0:
```python
import functools

import jax
import jax.numpy as jnp
import numpy as np
from jax import lax
from jax.experimental import pallas as pl
from jax.experimental.pallas import tpu as pltpu
from jax.sharding import PartitionSpec as P

NPTS = 8
FAR = 4
MESH = pl.DeviceIdType.MESH
F32, BF16, I32 = jnp.float32, jnp.bfloat16, jnp.int32


def legendre_table(points, degree):
    table = [np.ones(points.shape), points.copy()]
    for order in range(2, degree + 1):
        table.append(
            ((2 * order - 1) * points * table[order - 1] - (order - 1) * table[order - 2]) / order
        )
    return table


def lobatto_points(degree):
    points = np.cos(np.pi * np.arange(degree + 1) / degree)
    for sweep in range(100):
        table = legendre_table(points, degree)
        points = points - (points * table[degree] - table[degree - 1]) / (
            (degree + 1) * table[degree]
        )
    points = np.sort(points)
    return (points, legendre_table(points, degree)[degree])


def node_tables(count):
    degree = count - 1
    points, legendre = lobatto_points(degree)
    weights = 2.0 / (degree * (degree + 1) * legendre**2)
    spread = points[:, None] - points[None, :] + np.eye(count)
    derivative = legendre[:, None] / (legendre[None, :] * spread) * (1.0 - np.eye(count))
    derivative[0, 0] = -degree * (degree + 1) / 4.0
    derivative[degree, degree] = degree * (degree + 1) / 4.0
    halves = []
    for side in range(2):
        target = (points + 2.0 * side - 1.0) / 2.0
        matrix = np.ones((count, count))
        for column in range(count):
            for other in range(count):
                if other != column:
                    matrix[:, column] = (
                        matrix[:, column]
                        * (target - points[other])
                        / (points[column] - points[other])
                    )
        halves.append(matrix)
    return (points, weights, derivative, np.stack(halves))


POINTS, WEIGHTS, DERIV, HALVES = node_tables(NPTS)


def up(count, unit=8):
    return -(-count // unit) * unit


def halves_of(values):
    high = values.astype(BF16)
    return high, (values - high.astype(F32)).astype(BF16)


def numpy_halves(matrix):
    matrix = np.asarray(matrix, np.float32)
    high = matrix.astype(jnp.bfloat16)
    low = (matrix - high.astype(np.float32)).astype(jnp.bfloat16)
    return high, low


def dot(a, b, dims=((1,), (0,))):
    return lax.dot_general(a, b, (dims, ((), ())), preferred_element_type=F32)


def select(hot, values):
    high, low = halves_of(values)
    return dot(hot, high) + dot(hot, low)


def take_rows(hot, face):
    high, low = halves_of(face)
    dims = ((1,), (1,))
    return dot(hot, high, dims) + dot(hot, low, dims)


def spread_rows(rows, hot):
    high, low = halves_of(rows.T)
    return dot(high, hot) + dot(low, hot)


def product(a, matrix):
    high, low = halves_of(a)
    mhigh, mlow = halves_of(matrix)
    return dot(high, mhigh) + dot(low, mhigh) + dot(high, mlow)


def column(row, padded):
    count = row.shape[1]
    r = lax.broadcasted_iota(I32, (padded, count), 0)
    c = lax.broadcasted_iota(I32, (padded, count), 1)
    spread = jnp.where(r == c, jnp.broadcast_to(row.astype(F32), (padded, count)), 0.0)
    col = jnp.sum(spread, axis=1, keepdims=True)
    inside = lax.broadcasted_iota(I32, (padded, 1), 0) < count
    return jnp.where(inside, col, -1.0)


def hot_rows(columns, base, elems, kind=BF16):
    col = columns[0] if len(columns) == 1 else jnp.concatenate(columns, axis=0)
    lane = lax.broadcasted_iota(I32, (col.shape[0], elems), 1).astype(F32)
    return jnp.where(lane == col - float(base), 1.0, 0.0).astype(kind)


def line(values, matrix):
    half = NPTS // 2
    even = [values[i] + values[NPTS - 1 - i] for i in range(half)]
    odd = [values[i] - values[NPTS - 1 - i] for i in range(half)]
    out = [None] * NPTS
    for a in range(half):
        p = q = None
        for i in range(half):
            s = float((matrix[a, i] + matrix[a, NPTS - 1 - i]) / 2)
            t = float((matrix[a, i] - matrix[a, NPTS - 1 - i]) / 2)
            p = even[i] * s if p is None else p + even[i] * s
            q = odd[i] * t if q is None else q + odd[i] * t
        out[a] = q + p
        out[NPTS - 1 - a] = q - p
    return out


def stencils():
    forth, back = np.kron(np.eye(16), DERIV), np.kron(np.eye(16), DERIV.T)
    ends = np.concatenate([back[0::NPTS], back[NPTS - 1 :: NPTS]], axis=0)
    pieces = [piece for table in (forth, back, ends) for piece in numpy_halves(table)]
    return np.concatenate(pieces, axis=0)


def kernel(
    sizes,
    u_hbm,
    kappa_hbm,
    level_hbm,
    local_hbm,
    sub_hbm,
    near_hbm,
    far_hbm,
    child_hbm,
    coarse_hbm,
    deriv_hbm,
    mortar_hbm,
    peer_hbm,
    out_ref,
    level_ref,
    local_ref,
    sub_ref,
    near_ref,
    far_ref,
    child_ref,
    coarse_ref,
    deriv_ref,
    mortar_ref,
    peer_ref,
    w_ref,
    u_ref,
    k_ref,
    g_ref,
    y_ref,
    side_out,
    side_in,
    msg_out,
    msg_in,
    small_sem,
    load_sem,
    side_send,
    side_recv,
    msg_send,
    msg_recv,
):
    n_dom, n_sub = sizes
    parts = u_ref.shape[0]
    elems = parts * 128
    me, sub = lax.axis_index("dom"), lax.axis_index("sub")

    small = [
        pltpu.make_async_copy(source, target, small_sem.at[slot])
        for slot, (source, target) in enumerate(
            [
                (local_hbm, local_ref),
                (sub_hbm, sub_ref),
                (near_hbm, near_ref),
                (far_hbm, far_ref),
                (child_hbm, child_ref),
                (coarse_hbm, coarse_ref),
                (level_hbm, level_ref),
                (deriv_hbm, deriv_ref),
                (mortar_hbm, mortar_ref),
                (peer_hbm, peer_ref),
            ]
        )
    ]
    block = 128
    blocks = NPTS**3 // block

    def load(n, part, source, target, slot):
        own = pl.ds(part * block, block)
        return pltpu.make_async_copy(
            source.at[own, pl.ds(n * 128, 128)], target.at[n, own], load_sem.at[slot, n, part]
        )

    for copy in small[:7] + small[9:]:
        copy.start()
    small[7].start()
    for part in range(blocks):
        for n in range(parts):
            load(n, part, u_hbm, u_ref, 0).start()
            load(n, part, kappa_hbm, k_ref, 1).start()
    small[8].start()

    barrier = pltpu.get_barrier_semaphore()

    def greet(step, carry):
        other = lax.rem(me + step, n_dom)
        pl.semaphore_signal(barrier, inc=1, device_id=(other, sub), device_id_type=MESH)
        return carry

    lax.fori_loop(1, n_dom, greet, 0, unroll=n_dom <= 8)

    @pl.when(sub > 0)
    def _():
        pl.semaphore_signal(barrier, inc=1, device_id=(me, sub - 1), device_id_type=MESH)

    @pl.when(sub < n_sub - 1)
    def _():
        pl.semaphore_signal(barrier, inc=1, device_id=(me, sub + 1), device_id_type=MESH)

    def clear(missing, slot):
        @pl.when(missing)
        def _():
            side_in[slot] = jnp.zeros(side_in.shape[1:], F32)

    clear(sub == 0, 0)
    clear(sub == n_sub - 1, 1)
    clear(me == 0, 2)
    clear(me == n_dom - 1, 3)
    msg_in[me] = jnp.zeros(msg_in.shape[1:], F32)

    for copy in small[:7] + small[9:]:
        copy.wait()

    pairs, rim, near = local_ref.shape[1], sub_ref.shape[1], near_ref.shape[1]
    far, groups = far_ref.shape[1], child_ref.shape[1]
    farp, groupp, coarsep = up(far), up(groups), up(n_dom)
    hot0l = hot_rows([column(local_ref[1:2], up(pairs))], 0, elems)
    hot1l = hot_rows([column(local_ref[0:1], up(pairs))], elems, elems)
    hot0s = hot_rows([column(sub_ref[0:1], up(rim))], 0, elems)
    hot1s = hot_rows([column(sub_ref[1:2], up(rim))], elems, elems)
    hot2 = hot_rows([column(near_ref[0:1], up(near))], 2 * elems, elems)
    hot3 = hot_rows([column(near_ref[1:2], up(near))], 3 * elems, elems)
    children = [column(child_ref[m : m + 1], groupp) for m in range(4)]
    hot4f = hot_rows([column(far_ref[0:1], farp)] + children, 4 * elems, elems, F32)
    hot5f = hot_rows(
        [column(far_ref[1:2], farp), column(coarse_ref[...], coarsep)], 5 * elems, elems, F32
    )
    hot4, hot5, hot_kids = hot4f.astype(BF16), hot5f.astype(BF16), hot4f[farp:].astype(BF16)

    sources = 2 * farp + groupp + coarsep
    rows = 8 * n_dom

    def keys(shape, dim, group_slot, coarse_slot):
        c = lax.broadcasted_iota(I32, shape, dim)
        h = c - farp
        f = jnp.where(c < farp, c, h)
        s, j = lax.shift_right_logical(f, 2), lax.bitwise_and(f, FAR - 1)
        gap = jnp.where(c < farp, -2 - s, s + 2)
        key = jnp.where(f < far, (me + gap) * 8 + j, -1)
        key = jnp.where(c >= 2 * farp, -1, key)
        first = 2 * farp + groupp
        key = jnp.where(c >= first, (c - first) * 8 + coarse_slot, key)
        for slot in range(groups):
            key = jnp.where(c == 2 * farp + slot, peer_ref[slot] * 8 + group_slot, key)
        return key

    def hot(mask):
        return jnp.where(mask, 1.0, 0.0).astype(BF16)

    row = lax.broadcasted_iota(I32, (rows, sources), 0)
    route = hot(row == keys((1, sources), 1, 4, 5))
    origin = hot(row == keys((1, sources), 1, 5, 4))

    def rows_at(first, values):
        pieces = []
        if first:
            pieces.append(jnp.zeros((first, elems), F32))
        pieces.append(values)
        if first + values.shape[0] < sources:
            pieces.append(jnp.zeros((sources - first - values.shape[0], elems), F32))
        return pieces[0] if len(pieces) == 1 else jnp.concatenate(pieces, axis=0)

    def land(where, values):
        return dot(where, values.astype(BF16)).astype(BF16)

    at_five = rows_at(farp, hot5f[0:farp]) + rows_at(2 * farp + groupp, hot5f[farp:])
    send5 = land(route, at_five)
    send4 = [dot(route, rows_at(0, hot4f[0:farp]).astype(BF16))]
    dom_row = lax.broadcasted_iota(I32, (n_dom, groupp), 0)
    dom_slot = lax.broadcasted_iota(I32, (n_dom, groupp), 1)
    named = jnp.full((n_dom, groupp), -1, I32)
    for slot in range(groups):
        named = jnp.where(dom_slot == slot, peer_ref[slot], named)
    named = hot(named == dom_row)
    for m in range(4):
        first = farp + m * groupp
        send4.append(dot(named, hot4f[first : first + groupp].astype(BF16)))
    send4 = jnp.concatenate(send4, axis=0).astype(BF16)

    scale = jnp.exp2(-level_ref[...].astype(F32))
    sub8 = lax.broadcasted_iota(I32, (8, elems), 0)
    weight = jnp.zeros((8, elems), F32)
    for k in range(NPTS):
        weight = jnp.where(sub8 == k, float(WEIGHTS[k]), weight)
    weight = weight * scale

    def slab(i, j):
        return pl.ds((i * NPTS + j) * NPTS, NPTS)

    def across(ref, own):
        return jnp.concatenate([ref[n, own, :] for n in range(parts)], axis=1)

    def add_across(own, values):
        for n in range(parts):
            w_ref[n, own, :] += values[:, n * 128 : (n + 1) * 128]

    small[7].wait()
    turns = [deriv_ref[128 * n : 128 * n + 128, :] for n in range(4)]
    ends = [deriv_ref[512 + 32 * n : 544 + 32 * n, :] for n in range(2)]

    def along(pair, values):
        high, low = halves_of(values)
        both = jnp.concatenate([high, low], axis=0)
        return dot(jnp.concatenate([pair[0], pair[0]], axis=1), both) + dot(pair[1], high)

    low_face, high_face = [], []
    for part in range(blocks):
        own = pl.ds(part * block, block)
        if part == 0:
            for n in range(blocks * parts):
                load(n // blocks, n % blocks, u_hbm, u_ref, 0).wait()
                load(n // blocks, n % blocks, kappa_hbm, k_ref, 1).wait()
        if part == 0:
            small[8].wait()
        for n in range(parts):
            here = weight[:, n * 128 : (n + 1) * 128]
            for i in range(part * 2, part * 2 + 2):
                for j in range(NPTS):
                    g_ref[n, slab(i, j), :] = k_ref[n, slab(i, j), :] * (
                        here * float(WEIGHTS[i] * WEIGHTS[j])
                    )
        flux = along(turns[0:2], across(u_ref, own)) * across(g_ref, own)
        for n in range(parts):
            y_ref[n, own, :] = flux[:, n * 128 : (n + 1) * 128]
        end = along(ends, flux)
        low_face.append(end[0:16])
        high_face.append(end[16:32])

    square = NPTS * NPTS
    last = NPTS - 1
    low_i, high_i = pl.ds(0, square), pl.ds(last * square, square)
    low_k, high_k = pl.ds(0, square, NPTS), pl.ds(last, square, NPTS)
    u4, u5, g4, g5 = (across(r, k) for r in (u_ref, g_ref) for k in (low_k, high_k))
    flux = along(turns[0:2], jnp.concatenate([u4, u5], axis=0))
    flux = along(turns[2:4], flux * jnp.concatenate([g4, g5], axis=0))

    def across_i(u, g):
        part = line([u[i * NPTS : (i + 1) * NPTS] for i in range(NPTS)], DERIV)
        part = [part[i] * g[i * NPTS : (i + 1) * NPTS] for i in range(NPTS)]
        return jnp.concatenate(line(part, DERIV.T), axis=0)

    face4 = jnp.concatenate(low_face, axis=0) + flux[0:square] + across_i(u4, g4)
    face5 = jnp.concatenate(high_face, axis=0) + flux[square:] + across_i(u5, g5)

    down = [mortar_ref[m * square : (m + 1) * square, 0:square] for m in range(4)]
    lift = [mortar_ref[m * square : (m + 1) * square, square:] for m in range(4)]
    message = take_rows(send5, face5)
    taken4 = take_rows(send4, face4)
    message += taken4[0:rows]
    kids = [taken4[rows + m * n_dom : rows + (m + 1) * n_dom] for m in range(4)]
    sent = sum(product(kids[m], down[m]) for m in range(4))
    for p in range(n_dom):
        msg_out[p, :, 0:square] = message[8 * p : 8 * p + 8]
        msg_out[p, 4:5, 0:square] = sent[p : p + 1]

    pl.semaphore_wait(
        barrier, n_dom - 1 + (sub > 0).astype(I32) + (sub < n_sub - 1).astype(I32)
    )

    def post(step):
        other = lax.rem(me + step, n_dom)
        return pltpu.make_async_remote_copy(
            src_ref=msg_out.at[other],
            dst_ref=msg_in.at[me],
            send_sem=msg_send.at[other],
            recv_sem=msg_recv.at[me],
            device_id=(other, sub),
            device_id_type=MESH,
        )

    def arrival(step):
        other = lax.rem(me + step, n_dom)
        return pltpu.make_async_remote_copy(
            src_ref=msg_out.at[other],
            dst_ref=msg_in.at[other],
            send_sem=msg_send.at[other],
            recv_sem=msg_recv.at[other],
            device_id=(other, sub),
            device_id_type=MESH,
        )

    sides = [
        (sub > 0, 0, 1, (me, sub - 1)),
        (sub < n_sub - 1, 1, 0, (me, sub + 1)),
        (me > 0, 2, 3, (me - 1, sub)),
        (me < n_dom - 1, 3, 2, (me + 1, sub)),
    ]

    def side_copy(mine, theirs, device):
        return pltpu.make_async_remote_copy(
            src_ref=side_out.at[mine],
            dst_ref=side_in.at[theirs],
            send_sem=side_send.at[mine],
            recv_sem=side_recv.at[theirs],
            device_id=device,
            device_id_type=MESH,
        )

    def start_all(step, carry):
        post(step).start()
        return carry

    lax.fori_loop(1, n_dom, start_all, 0, unroll=n_dom <= 8)

    for part in range(blocks):
        own = pl.ds(part * block, block)
        turn = along(turns[2:4], across(y_ref, own))
        for n in range(parts):
            w_ref[n, own, :] = turn[:, n * 128 : (n + 1) * 128]
    for n in range(parts):
        for j in range(NPTS):
            flux = line([u_ref[n, slab(i, j), :] for i in range(NPTS)], DERIV)
            flux = [flux[i] * g_ref[n, slab(i, j), :] for i in range(NPTS)]
            flux = line(flux, DERIV.T)
            for i in range(NPTS):
                w_ref[n, slab(i, j), :] += flux[i]
        for i in range(NPTS):
            flux = line([u_ref[n, slab(i, j), :] for j in range(NPTS)], DERIV)
            flux = [flux[j] * g_ref[n, slab(i, j), :] for j in range(NPTS)]
            flux = line(flux, DERIV.T)
            for j in range(NPTS):
                w_ref[n, slab(i, j), :] += flux[j]
    face0 = across(w_ref, low_i)
    face1 = across(w_ref, high_i)
    face2 = jnp.concatenate([across(w_ref, slab(i, 0)) for i in range(NPTS)], axis=0)
    face3 = jnp.concatenate([across(w_ref, slab(i, last)) for i in range(NPTS)], axis=0)
    side_out[0, 0:rim, 0:square] = take_rows(hot0s, face0)[0:rim]
    side_out[1, 0:rim, 0:square] = take_rows(hot1s, face1)[0:rim]
    side_out[2, 0:near, 0:square] = take_rows(hot2, face2)[0:near]
    side_out[3, 0:near, 0:square] = take_rows(hot3, face3)[0:near]

    for there, mine, theirs, device in sides:
        @pl.when(there)
        def _():
            side_copy(mine, theirs, device).start()

    taken4 = take_rows(hot_kids, face4)
    family = [taken4[m * groupp : (m + 1) * groupp] for m in range(4)]
    projected = sum(product(family[m], down[m]) for m in range(4))

    land4 = land(origin, rows_at(0, hot4f[0:farp]))
    land5 = land(origin, at_five)
    first = farp
    land_kids = []
    for m in range(4):
        land_kids.append(land(origin, rows_at(2 * farp, hot4f[first : first + groupp])))
        first += groupp

    share = [product(projected, lift[m]) - family[m] for m in range(4)]
    add_across(low_k, spread_rows(jnp.concatenate(share, axis=0), hot_kids))

    kron = halves_of(mortar_ref[:, 0:square])

    add_across(low_i, spread_rows(take_rows(hot1l, face1), hot0l))
    add_across(high_i, spread_rows(take_rows(hot0l, face0), hot1l))

    for there, mine, theirs, device in sides:
        @pl.when(there)
        def _():
            side_copy(mine, mine, device).wait()

    add_across(low_i, spread_rows(side_in[0, 0:rim, 0:square], hot0s))
    add_across(high_i, spread_rows(side_in[1, 0:rim, 0:square], hot1s))
    add2 = spread_rows(side_in[2, 0:near, 0:square], hot2)
    add3 = spread_rows(side_in[3, 0:near, 0:square], hot3)
    for i in range(NPTS):
        add_across(slab(i, 0), add2[i * NPTS : (i + 1) * NPTS])
        add_across(slab(i, last), add3[i * NPTS : (i + 1) * NPTS])

    def wait_all(step, carry):
        arrival(step).wait()
        return carry

    lax.fori_loop(1, n_dom, wait_all, 0, unroll=n_dom <= 8)
    received = jnp.concatenate([msg_in[p, :, 0:square] for p in range(n_dom)], axis=0)
    high, low = halves_of(received.T)
    add5 = dot(high, land5) + dot(low, land5)
    add4 = dot(high, land4) + dot(low, land4)
    lifted = dot(kron[0], high) + dot(kron[0], low) + dot(kron[1], high)
    for m in range(4):
        high, low = halves_of(lifted[m * square : (m + 1) * square])
        add4 += dot(high, land_kids[m]) + dot(low, land_kids[m])
    add_across(high_k, add5)
    add_across(low_k, add4)
    for n in range(parts):
        out_ref[:, n * 128 : (n + 1) * 128] = w_ref[n]


def body(
    sizes,
    nodal_values,
    kappa,
    levels,
    local_faces,
    sub_faces,
    near_faces,
    far_faces,
    child_faces,
    child_peer,
    coarse_faces,
):
    n_dom, n_sub = sizes
    elems = nodal_values.shape[1]
    krons = [np.kron(HALVES[m // 2], HALVES[m % 2]) for m in range(4)]
    mortar = np.concatenate([np.concatenate([m, m.T], axis=1) for m in krons], axis=0)
    held = (elems // 128, NPTS**3, 128)
    side_rows = up(max(sub_faces.shape[1], near_faces.shape[1]))
    small = [
        levels.reshape(1, elems),
        local_faces,
        sub_faces,
        near_faces,
        far_faces,
        child_faces,
        coarse_faces.reshape(1, n_dom),
        jnp.asarray(stencils(), BF16),
        jnp.asarray(mortar, F32),
    ]
    hbm = pl.BlockSpec(memory_space=pltpu.HBM)
    vmem = pl.BlockSpec(memory_space=pltpu.VMEM)
    return pl.pallas_call(
        functools.partial(kernel, sizes),
        out_shape=pltpu.VMEM(nodal_values.shape, F32),
        in_specs=[hbm] * 12,
        out_specs=vmem,
        scratch_shapes=[pltpu.VMEM(item.shape, item.dtype) for item in small]
        + [
            pltpu.SMEM(child_peer.shape, I32),
            pltpu.VMEM(held, F32),
            pltpu.VMEM(held, F32),
            pltpu.VMEM(held, F32),
            pltpu.VMEM(held, F32),
            pltpu.VMEM(held, F32),
            pltpu.VMEM((4, side_rows, 128), F32),
            pltpu.VMEM((4, side_rows, 128), F32),
            pltpu.VMEM((n_dom, 8, 128), F32),
            pltpu.VMEM((n_dom, 8, 128), F32),
            pltpu.SemaphoreType.DMA((len(small) + 1,)),
            pltpu.SemaphoreType.DMA((2, held[0], NPTS**3 // 128)),
            pltpu.SemaphoreType.DMA((4,)),
            pltpu.SemaphoreType.DMA((4,)),
            pltpu.SemaphoreType.DMA((n_dom,)),
            pltpu.SemaphoreType.DMA((n_dom,)),
        ],
        compiler_params=pltpu.CompilerParams(
            collective_id=0, has_side_effects=True, vmem_limit_bytes=60 * 1024 * 1024
        ),
    )(
        nodal_values,
        kappa,
        *small,
        child_peer,
    )


def solution(mesh):
    sizes = (mesh.shape["dom"], mesh.shape["sub"])
    wide = P(None, ("dom", "sub"))
    flat = P(("dom", "sub"))
    in_specs = (wide, wide, flat, wide, wide, wide, wide, wide, flat, flat)
    return jax.shard_map(
        functools.partial(body, sizes),
        mesh=mesh,
        in_specs=in_specs,
        out_specs=wide,
        check_vma=False,
    )
```

profile of v0, /device:TPU:0, one launch (start us, length us, event | category | flops | bytes accessed | tf_op | source)
XLA Modules:
  0.0 12.7 jit_solution(3558205820539622781)
XLA Ops:
  0.0 11.9 %shard_map.118 = f32[512,256]{1,0:T(8,128)S(1)} custom-call(f32[512,256]{1,0:T(8,128)} %u_hbm.1, f32[512,256]{1,0:T(8,128)} %kappa_hbm.1, s32[1,256]{1,0:T(1,128)} %bitcast.2, s32[2,64]{1,0:T(2,128)} %local_hbm.1, s32[2,32]{1,0:T(2,128)} %sub_hbm.1, s32[2,32]{1,0:T(2,128)} %near_hbm.1, s32[2,12]{1,0:T(2,128)} %far_hbm.1, s32[4,3]{1,0:T(4,128)} %child_hbm.1, ...), custom_call_target="tpu_custom_call" | custom-call | tf_op jit(solution)/shard_map/pallas_call | solution.py:565
  11.9 0.8 %copy.14 = f32[512,256]{1,0:T(8,128)} copy(f32[512,256]{1,0:T(8,128)S(1)} %shard_map.118) | data formatting | bytes 1048576
where the time goes:
time: 12.8 us; the launch traced here: 12.7 us
  Pallas kernels  11.9 us (93%)
  local copies, waits for them, and re-layouts  0.8 us (6%)
    pallas_call x1, Pallas kernels, body(): pl.pallas_call(functools.partial(kernel, sizes), out_shape=pltpu.VMEM(nod...  11.9 us
    unnamed x1, local copies, waits for them, and re-layouts  0.8 us

commit v1 on v0

v1 whole, which is shorter than its diff:
```python
import functools

import jax
import jax.numpy as jnp
import numpy as np
from jax import lax
from jax.experimental import pallas as pl
from jax.experimental.pallas import tpu as pltpu
from jax.sharding import PartitionSpec as P

NPTS = 8
FAR = 4
MESH = pl.DeviceIdType.MESH
F32, BF16, I32 = jnp.float32, jnp.bfloat16, jnp.int32


def legendre_table(points, degree):
    table = [np.ones(points.shape), points.copy()]
    for order in range(2, degree + 1):
        table.append(
            ((2 * order - 1) * points * table[order - 1] - (order - 1) * table[order - 2]) / order
        )
    return table


def lobatto_points(degree):
    points = np.cos(np.pi * np.arange(degree + 1) / degree)
    for sweep in range(100):
        table = legendre_table(points, degree)
        points = points - (points * table[degree] - table[degree - 1]) / (
            (degree + 1) * table[degree]
        )
    points = np.sort(points)
    return (points, legendre_table(points, degree)[degree])


def node_tables(count):
    degree = count - 1
    points, legendre = lobatto_points(degree)
    weights = 2.0 / (degree * (degree + 1) * legendre**2)
    spread = points[:, None] - points[None, :] + np.eye(count)
    derivative = legendre[:, None] / (legendre[None, :] * spread) * (1.0 - np.eye(count))
    derivative[0, 0] = -degree * (degree + 1) / 4.0
    derivative[degree, degree] = degree * (degree + 1) / 4.0
    halves = []
    for side in range(2):
        target = (points + 2.0 * side - 1.0) / 2.0
        matrix = np.ones((count, count))
        for column in range(count):
            for other in range(count):
                if other != column:
                    matrix[:, column] = (
                        matrix[:, column]
                        * (target - points[other])
                        / (points[column] - points[other])
                    )
        halves.append(matrix)
    return (points, weights, derivative, np.stack(halves))


POINTS, WEIGHTS, DERIV, HALVES = node_tables(NPTS)


def up(count, unit=8):
    return -(-count // unit) * unit


def halves_of(values):
    high = values.astype(BF16)
    return high, (values - high.astype(F32)).astype(BF16)


def numpy_halves(matrix):
    matrix = np.asarray(matrix, np.float32)
    high = matrix.astype(jnp.bfloat16)
    low = (matrix - high.astype(np.float32)).astype(jnp.bfloat16)
    return high, low


def dot(a, b, dims=((1,), (0,))):
    return lax.dot_general(a, b, (dims, ((), ())), preferred_element_type=F32)


def select(hot, values):
    high, low = halves_of(values)
    return dot(hot, high) + dot(hot, low)


def take_rows(hot, face):
    high, low = halves_of(face)
    dims = ((1,), (1,))
    return dot(hot, high, dims) + dot(hot, low, dims)


def spread_rows(rows, hot):
    high, low = halves_of(rows.T)
    return dot(high, hot) + dot(low, hot)


def product(a, matrix):
    high, low = halves_of(a)
    mhigh, mlow = halves_of(matrix)
    return dot(high, mhigh) + dot(low, mhigh) + dot(high, mlow)


def column(row, padded):
    count = row.shape[1]
    r = lax.broadcasted_iota(I32, (padded, count), 0)
    c = lax.broadcasted_iota(I32, (padded, count), 1)
    spread = jnp.where(r == c, jnp.broadcast_to(row.astype(F32), (padded, count)), 0.0)
    col = jnp.sum(spread, axis=1, keepdims=True)
    inside = lax.broadcasted_iota(I32, (padded, 1), 0) < count
    return jnp.where(inside, col, -1.0)


def hot_rows(columns, base, elems, kind=BF16):
    col = columns[0] if len(columns) == 1 else jnp.concatenate(columns, axis=0)
    lane = lax.broadcasted_iota(I32, (col.shape[0], elems), 1).astype(F32)
    return jnp.where(lane == col - float(base), 1.0, 0.0).astype(kind)


def line(values, matrix):
    half = NPTS // 2
    even = [values[i] + values[NPTS - 1 - i] for i in range(half)]
    odd = [values[i] - values[NPTS - 1 - i] for i in range(half)]
    out = [None] * NPTS
    for a in range(half):
        p = q = None
        for i in range(half):
            s = float((matrix[a, i] + matrix[a, NPTS - 1 - i]) / 2)
            t = float((matrix[a, i] - matrix[a, NPTS - 1 - i]) / 2)
            p = even[i] * s if p is None else p + even[i] * s
            q = odd[i] * t if q is None else q + odd[i] * t
        out[a] = q + p
        out[NPTS - 1 - a] = q - p
    return out


def stencils():
    forth, back = np.kron(np.eye(16), DERIV), np.kron(np.eye(16), DERIV.T)
    pieces = [piece for table in (forth, back) for piece in numpy_halves(table)]
    return np.concatenate(pieces, axis=0)


def folds(krons):
    one = np.eye(NPTS)
    apply = np.concatenate(
        [np.kron(one, one), np.kron(DERIV.T, one), np.kron(one, DERIV.T)], axis=1
    )
    heads = [np.eye(NPTS * NPTS)] * 2 + [m.T for m in krons] + krons
    table = np.concatenate([(head @ apply).T for head in heads], axis=1)
    return np.concatenate(numpy_halves(table), axis=0)


def kernel(
    sizes,
    u_hbm,
    kappa_hbm,
    level_hbm,
    local_hbm,
    sub_hbm,
    near_hbm,
    far_hbm,
    child_hbm,
    coarse_hbm,
    fold_hbm,
    deriv_hbm,
    mortar_hbm,
    peer_hbm,
    out_ref,
    level_ref,
    local_ref,
    sub_ref,
    near_ref,
    far_ref,
    child_ref,
    coarse_ref,
    fold_ref,
    deriv_ref,
    mortar_ref,
    peer_ref,
    w_ref,
    u_ref,
    k_ref,
    g_ref,
    side_out,
    side_in,
    far_out,
    far_in,
    mort_out,
    mort_in,
    small_sem,
    load_sem,
    side_send,
    side_recv,
    far_send,
    far_recv,
    mort_send,
    mort_recv,
):
    n_dom, n_sub = sizes
    parts = u_ref.shape[0]
    elems = parts * 128
    square = NPTS * NPTS
    last = NPTS - 1
    me, sub = lax.axis_index("dom"), lax.axis_index("sub")

    urgent = [
        (far_hbm, far_ref),
        (child_hbm, child_ref),
        (coarse_hbm, coarse_ref),
        (level_hbm, level_ref),
        (peer_hbm, peer_ref),
    ]
    later = [
        (fold_hbm, fold_ref),
        (local_hbm, local_ref),
        (sub_hbm, sub_ref),
        (near_hbm, near_ref),
        (deriv_hbm, deriv_ref),
        (mortar_hbm, mortar_ref),
    ]
    small = [
        pltpu.make_async_copy(source, target, small_sem.at[slot])
        for slot, (source, target) in enumerate(urgent + later)
    ]
    block = 128
    blocks = NPTS**3 // block

    def load(n, part, source, target, slot):
        own = pl.ds(part * block, block)
        return pltpu.make_async_copy(
            source.at[own, pl.ds(n * 128, 128)], target.at[n, own], load_sem.at[slot, n, part]
        )

    for copy in small[:5]:
        copy.start()
    for part in range(blocks):
        for n in range(parts):
            load(n, part, u_hbm, u_ref, 0).start()
            load(n, part, kappa_hbm, k_ref, 1).start()
    for copy in small[5:]:
        copy.start()

    far_in[...] = jnp.zeros(far_in.shape, F32)
    mort_in[...] = jnp.zeros(mort_in.shape, F32)

    barrier = pltpu.get_barrier_semaphore()

    def greet(step, carry):
        other = lax.rem(me + step, n_dom)
        pl.semaphore_signal(barrier, inc=1, device_id=(other, sub), device_id_type=MESH)
        return carry

    lax.fori_loop(1, n_dom, greet, 0, unroll=n_dom <= 8)

    @pl.when(sub > 0)
    def _():
        pl.semaphore_signal(barrier, inc=1, device_id=(me, sub - 1), device_id_type=MESH)

    @pl.when(sub < n_sub - 1)
    def _():
        pl.semaphore_signal(barrier, inc=1, device_id=(me, sub + 1), device_id_type=MESH)

    def clear(missing, slot):
        @pl.when(missing)
        def _():
            side_in[slot] = jnp.zeros(side_in.shape[1:], F32)

    clear(sub == 0, 0)
    clear(sub == n_sub - 1, 1)
    clear(me == 0, 2)
    clear(me == n_dom - 1, 3)

    pairs, rim, near = local_ref.shape[1], sub_ref.shape[1], near_ref.shape[1]
    far, groups = far_ref.shape[1], child_ref.shape[1]
    shifts = far // FAR
    farp, groupp, coarsep = up(far), up(groups), up(n_dom)
    coarse_at = 2 * farp
    kids_at = coarse_at + coarsep
    used = kids_at + 4 * groupp
    sources = up(used, 128)
    lane = lax.broadcasted_iota(I32, (8, sources), 1)
    row8 = lax.broadcasted_iota(I32, (8, sources), 0)
    on_low = (lane < farp) | (lane >= kids_at)
    on_low_plane = jnp.concatenate([on_low] * NPTS, axis=0)
    reach = [
        jnp.where(on_low, float(WEIGHTS[c] * DERIV[c, 0]), float(WEIGHTS[c] * DERIV[c, last]))
        for c in range(NPTS)
    ]
    turn8 = []
    for r in range(NPTS):
        table = jnp.zeros((8, sources), F32)
        for b in range(NPTS):
            table = jnp.where(row8 == b, float(DERIV[b, (b + r) % NPTS]), table)
        turn8.append(table)
    quad8 = jnp.zeros((8, sources), F32)
    for k in range(NPTS):
        quad8 = jnp.where(row8 == k, float(WEIGHTS[k]), quad8)

    for copy in small[:5]:
        copy.wait()

    columns = [
        column(far_ref[0:1], farp) - float(4 * elems),
        column(far_ref[1:2], farp) - float(5 * elems),
        column(coarse_ref[...], coarsep) - float(5 * elems),
    ] + [column(child_ref[m : m + 1], groupp) - float(4 * elems) for m in range(4)]
    columns.append(jnp.full((sources - used, 1), -1.0, F32))
    hot_src = hot_rows(columns, 0, elems)

    scale = jnp.exp2(-level_ref[...].astype(F32))
    over = ((1,), (1,))
    chosen = dot(jnp.broadcast_to(scale, (16, elems)).astype(BF16), hot_src, over)[0:8]
    chosen = chosen * quad8

    for n in range(blocks * parts):
        load(n // blocks, n % blocks, u_hbm, u_ref, 0).wait()
        load(n // blocks, n % blocks, kappa_hbm, k_ref, 1).wait()

    def pick(ref, k):
        own = pl.ds(k, square, NPTS)
        high, low = halves_of(jnp.concatenate([ref[n, own, :] for n in range(parts)], axis=1))
        return dot(high, hot_src, over) + dot(low, hot_src, over)

    order = [0, last] + list(range(1, last))
    u_of, k_of = [None] * NPTS, [None] * NPTS
    for k in order:
        u_of[k], k_of[k] = pick(u_ref, k), pick(k_ref, k)
    u_plane = jnp.where(on_low_plane, u_of[0], u_of[last])
    k_plane = jnp.where(on_low_plane, k_of[0], k_of[last])

    def strip(plane, i):
        return plane[i * NPTS : (i + 1) * NPTS]

    edge = float(WEIGHTS[0])
    up_i = line([strip(u_plane, i) for i in range(NPTS)], DERIV)
    along_k, along_i, along_j = [], [], []
    for i in range(NPTS):
        here = chosen * float(WEIGHTS[i])
        g = strip(k_plane, i) * (here * edge)
        along_i.append(up_i[i] * g)
        flat = strip(u_plane, i)
        turned = turn8[0] * flat
        for r in range(1, NPTS):
            turned += turn8[r] * pltpu.roll(flat, NPTS - r, 0)
        along_j.append(turned * g)
        deep = line([strip(u_of[k], i) for k in range(NPTS)], DERIV)
        total = reach[0] * strip(k_of[0], i) * deep[0]
        for c in range(1, NPTS):
            total += reach[c] * strip(k_of[c], i) * deep[c]
        along_k.append(total * here)
    flux = jnp.concatenate(along_k + along_i + along_j, axis=0).T

    small[5].wait()
    fold = fold_ref.shape[0] // 2

    def folded(rows, first, width):
        high, low = halves_of(rows)
        cols = pl.ds(first, width)
        return (
            dot(high, fold_ref[0:fold, cols])
            + dot(low, fold_ref[0:fold, cols])
            + dot(high, fold_ref[fold:, cols])
        )

    own = folded(flux[0:up(used, 16)], 0, 128)
    kids = folded(flux[kids_at:used], 128, 256)
    raised = folded(flux[coarse_at:kids_at], 384, 256)

    half = lax.broadcasted_iota(I32, (8, 128), 1) < square
    for side in range(2):
        for first in range(0, farp, 8):
            faces = own[side * farp + first : side * farp + first + 8]
            far_out[side, first : first + 8] = jnp.where(half, faces, pltpu.roll(faces, 6, 0))
    half_g = lax.broadcasted_iota(I32, (groupp, 128), 1) < square
    kid = [kids[m * groupp : (m + 1) * groupp] for m in range(4)]
    projected = jnp.where(half_g, kid[0][:, 0:128], kid[1][:, 0:128]) + jnp.where(
        half_g, kid[2][:, 128:256], kid[3][:, 128:256]
    )
    peer_row = lax.broadcasted_iota(I32, (n_dom, 128), 0)
    routed = jnp.zeros((n_dom, 128), F32)
    for slot in range(groups):
        routed = jnp.where(peer_row == peer_ref[slot], projected[slot : slot + 1], routed)
    mort_out[pl.ds(0, n_dom, 8), :] = routed
    mort_out[pl.ds(1, n_dom, 8), :] = raised[0:n_dom, 0:128]
    mort_out[pl.ds(2, n_dom, 8), :] = raised[0:n_dom, 128:256]

    greeted = n_dom - 1 + (sub > 0).astype(I32) + (sub < n_sub - 1).astype(I32)

    def mail(step, landing):
        other = lax.rem(me + step, n_dom)
        return pltpu.make_async_remote_copy(
            src_ref=mort_out.at[pl.ds(pl.multiple_of(other * 8, 8), 3)],
            dst_ref=mort_in.at[
                pl.ds(pl.multiple_of((other if landing else me) * 8, 8), 3)
            ],
            send_sem=mort_send.at[other],
            recv_sem=mort_recv.at[other if landing else me],
            device_id=(other, sub),
            device_id_type=MESH,
        )

    def far_copy(side, s, landing):
        other = me - s - 2 if side == 0 else me + s + 2
        rows = pl.ds(s * FAR, FAR // 2)
        there = side if landing else 1 - side
        return pltpu.make_async_remote_copy(
            src_ref=far_out.at[side, rows],
            dst_ref=far_in.at[there, rows],
            send_sem=far_send.at[side, s],
            recv_sem=far_recv.at[there, s],
            device_id=(other, sub),
            device_id_type=MESH,
        )

    def far_there(side, s):
        return me >= s + 2 if side == 0 else me + s + 2 < n_dom

    def send_messages():
        pl.semaphore_wait(barrier, greeted)

        def start_all(step, carry):
            mail(step, False).start()
            return carry

        lax.fori_loop(1, n_dom, start_all, 0, unroll=n_dom <= 8)
        for side in range(2):
            for s in range(shifts):
                @pl.when(far_there(side, s))
                def _():
                    far_copy(side, s, False).start()

    @pl.when(me > 0)
    def _():
        send_messages()

    for copy in small[6:]:
        copy.wait()

    hot0l = hot_rows([column(local_ref[1:2], up(pairs))], 0, elems)
    hot1l = hot_rows([column(local_ref[0:1], up(pairs))], elems, elems)
    hot0s = hot_rows([column(sub_ref[0:1], up(rim))], 0, elems)
    hot1s = hot_rows([column(sub_ref[1:2], up(rim))], elems, elems)
    hot2 = hot_rows([column(near_ref[0:1], up(near))], 2 * elems, elems)
    hot3 = hot_rows([column(near_ref[1:2], up(near))], 3 * elems, elems)

    sub8 = lax.broadcasted_iota(I32, (8, elems), 0)
    weight = jnp.zeros((8, elems), F32)
    for k in range(NPTS):
        weight = jnp.where(sub8 == k, float(WEIGHTS[k]), weight)
    weight = weight * scale

    def slab(i, j):
        return pl.ds((i * NPTS + j) * NPTS, NPTS)

    def across(ref, own):
        return jnp.concatenate([ref[n, own, :] for n in range(parts)], axis=1)

    def add_across(own, values):
        for n in range(parts):
            w_ref[n, own, :] += values[:, n * 128 : (n + 1) * 128]

    turns = [deriv_ref[128 * n : 128 * n + 128, :] for n in range(4)]

    def along(pair, values):
        high, low = halves_of(values)
        both = jnp.concatenate([high, low], axis=0)
        return dot(jnp.concatenate([pair[0], pair[0]], axis=1), both) + dot(pair[1], high)

    for n in range(parts):
        here = weight[:, n * 128 : (n + 1) * 128]
        for i in range(NPTS):
            for j in range(NPTS):
                g_ref[n, slab(i, j), :] = k_ref[n, slab(i, j), :] * (
                    here * float(WEIGHTS[i] * WEIGHTS[j])
                )
    for part in range(blocks):
        own_rows = pl.ds(part * block, block)
        turn = along(turns[0:2], across(u_ref, own_rows)) * across(g_ref, own_rows)
        turn = along(turns[2:4], turn)
        for n in range(parts):
            w_ref[n, own_rows, :] = turn[:, n * 128 : (n + 1) * 128]
    for n in range(parts):
        for j in range(NPTS):
            turn = line([u_ref[n, slab(i, j), :] for i in range(NPTS)], DERIV)
            turn = [turn[i] * g_ref[n, slab(i, j), :] for i in range(NPTS)]
            turn = line(turn, DERIV.T)
            for i in range(NPTS):
                w_ref[n, slab(i, j), :] += turn[i]
        for i in range(NPTS):
            turn = line([u_ref[n, slab(i, j), :] for j in range(NPTS)], DERIV)
            turn = [turn[j] * g_ref[n, slab(i, j), :] for j in range(NPTS)]
            turn = line(turn, DERIV.T)
            for j in range(NPTS):
                w_ref[n, slab(i, j), :] += turn[j]

    low_i, high_i = pl.ds(0, square), pl.ds(last * square, square)
    low_k, high_k = pl.ds(0, square, NPTS), pl.ds(last, square, NPTS)
    face0 = across(w_ref, low_i)
    face1 = across(w_ref, high_i)
    face2 = jnp.concatenate([across(w_ref, slab(i, 0)) for i in range(NPTS)], axis=0)
    face3 = jnp.concatenate([across(w_ref, slab(i, last)) for i in range(NPTS)], axis=0)
    side_out[0, 0:rim, 0:square] = take_rows(hot0s, face0)[0:rim]
    side_out[1, 0:rim, 0:square] = take_rows(hot1s, face1)[0:rim]
    side_out[2, 0:near, 0:square] = take_rows(hot2, face2)[0:near]
    side_out[3, 0:near, 0:square] = take_rows(hot3, face3)[0:near]

    @pl.when(me == 0)
    def _():
        send_messages()

    sides = [
        (sub > 0, 0, 1, (me, sub - 1)),
        (sub < n_sub - 1, 1, 0, (me, sub + 1)),
        (me > 0, 2, 3, (me - 1, sub)),
        (me < n_dom - 1, 3, 2, (me + 1, sub)),
    ]

    def side_copy(mine, theirs, device):
        return pltpu.make_async_remote_copy(
            src_ref=side_out.at[mine],
            dst_ref=side_in.at[theirs],
            send_sem=side_send.at[mine],
            recv_sem=side_recv.at[theirs],
            device_id=device,
            device_id_type=MESH,
        )

    for there, mine, theirs, device in sides:
        @pl.when(there)
        def _():
            side_copy(mine, theirs, device).start()

    keyed = up(2 * farp + 8 * n_dom, 128)

    def landing_rows(keys):
        at = lax.broadcasted_iota(I32, (2 * keyed, sources), 0)
        hit = at == keys[0]
        for key in keys[1:]:
            hit = hit | (at == key)
        return dot(jnp.where(hit, 1.0, 0.0).astype(BF16), hot_src).astype(BF16)

    src = lax.broadcasted_iota(I32, (1, sources), 1)

    def far_key(first):
        f = src - first
        s, j = lax.shift_right_logical(f, 2), lax.bitwise_and(f, FAR - 1)
        key = lax.shift_right_logical(j, 1) * keyed + first + 4 * s + lax.bitwise_and(j, 1)
        return jnp.where((f >= 0) & (f < far), key, -1)

    key4 = far_key(0)
    for m in range(4):
        for slot in range(groups):
            key = (m & 1) * keyed + 2 * farp + peer_ref[slot] * 8 + 1 + (m >> 1)
            key4 = jnp.where(src == kids_at + m * groupp + slot, key, key4)
    key5 = far_key(farp)
    p = src - coarse_at
    holds = (p >= 0) & (p < n_dom)
    key5 = jnp.where(holds, 2 * farp + 8 * p, key5)
    land4 = landing_rows([key4])
    land5 = landing_rows([key5, jnp.where(holds, keyed + 2 * farp + 8 * p, -1)])

    joined = projected[:, 0:square] + projected[:, square:]
    lift = [mortar_ref[m * square : (m + 1) * square, :] for m in range(4)]
    share = []
    for m in range(4):
        first = kids_at + m * groupp
        share.append(product(joined, lift[m]) - own[first : first + groupp, 0:square])
    hot_kids = hot_src[kids_at:used]
    add_across(low_k, spread_rows(jnp.concatenate(share, axis=0), hot_kids))
    add_across(low_i, spread_rows(take_rows(hot1l, face1), hot0l))
    add_across(high_i, spread_rows(take_rows(hot0l, face0), hot1l))

    for there, mine, theirs, device in sides:
        @pl.when(there)
        def _():
            side_copy(mine, mine, device).wait()

    add_across(low_i, spread_rows(side_in[0, 0:rim, 0:square], hot0s))
    add_across(high_i, spread_rows(side_in[1, 0:rim, 0:square], hot1s))
    add2 = spread_rows(side_in[2, 0:near, 0:square], hot2)
    add3 = spread_rows(side_in[3, 0:near, 0:square], hot3)
    for i in range(NPTS):
        add_across(slab(i, 0), add2[i * NPTS : (i + 1) * NPTS])
        add_across(slab(i, last), add3[i * NPTS : (i + 1) * NPTS])

    def wait_all(step, carry):
        mail(step, True).wait()
        return carry

    lax.fori_loop(1, n_dom, wait_all, 0, unroll=n_dom <= 8)
    for side in range(2):
        for s in range(shifts):
            @pl.when(far_there(side, s))
            def _():
                far_copy(side, s, True).wait()

    received = [far_in[0], far_in[1], mort_in[...]]
    spare = keyed - 2 * farp - 8 * n_dom
    if spare:
        received.append(jnp.zeros((spare, 128), F32))
    received = jnp.concatenate(received, axis=0).T
    received = jnp.concatenate([received[0:square], received[square:]], axis=1)
    high, low = halves_of(received)
    add_across(low_k, dot(high, land4) + dot(low, land4))
    add_across(high_k, dot(high, land5) + dot(low, land5))
    for n in range(parts):
        out_ref[:, n * 128 : (n + 1) * 128] = w_ref[n]


def body(
    sizes,
    nodal_values,
    kappa,
    levels,
    local_faces,
    sub_faces,
    near_faces,
    far_faces,
    child_faces,
    child_peer,
    coarse_faces,
):
    n_dom, n_sub = sizes
    elems = nodal_values.shape[1]
    krons = [np.kron(HALVES[m // 2], HALVES[m % 2]) for m in range(4)]
    mortar = np.concatenate([m.T for m in krons], axis=0)
    far_rows = up(far_faces.shape[1])
    held = (elems // 128, NPTS**3, 128)
    side_rows = up(max(sub_faces.shape[1], near_faces.shape[1]))
    small = [
        levels.reshape(1, elems),
        local_faces,
        sub_faces,
        near_faces,
        far_faces,
        child_faces,
        coarse_faces.reshape(1, n_dom),
        jnp.asarray(folds(krons), BF16),
        jnp.asarray(stencils(), BF16),
        jnp.asarray(mortar, F32),
    ]
    hbm = pl.BlockSpec(memory_space=pltpu.HBM)
    vmem = pl.BlockSpec(memory_space=pltpu.VMEM)
    return pl.pallas_call(
        functools.partial(kernel, sizes),
        out_shape=pltpu.VMEM(nodal_values.shape, F32),
        in_specs=[hbm] * 13,
        out_specs=vmem,
        scratch_shapes=[pltpu.VMEM(item.shape, item.dtype) for item in small]
        + [
            pltpu.SMEM(child_peer.shape, I32),
            pltpu.VMEM(held, F32),
            pltpu.VMEM(held, F32),
            pltpu.VMEM(held, F32),
            pltpu.VMEM(held, F32),
            pltpu.VMEM((4, side_rows, 128), F32),
            pltpu.VMEM((4, side_rows, 128), F32),
            pltpu.VMEM((2, far_rows, 128), F32),
            pltpu.VMEM((2, far_rows, 128), F32),
            pltpu.VMEM((n_dom * 8, 128), F32),
            pltpu.VMEM((n_dom * 8, 128), F32),
            pltpu.SemaphoreType.DMA((len(small) + 1,)),
            pltpu.SemaphoreType.DMA((2, held[0], NPTS**3 // 128)),
            pltpu.SemaphoreType.DMA((4,)),
            pltpu.SemaphoreType.DMA((4,)),
            pltpu.SemaphoreType.DMA((2, far_faces.shape[1] // FAR)),
            pltpu.SemaphoreType.DMA((2, far_faces.shape[1] // FAR)),
            pltpu.SemaphoreType.DMA((n_dom,)),
            pltpu.SemaphoreType.DMA((n_dom,)),
        ],
        compiler_params=pltpu.CompilerParams(
            collective_id=0, has_side_effects=True, vmem_limit_bytes=60 * 1024 * 1024
        ),
    )(
        nodal_values,
        kappa,
        *small,
        child_peer,
    )


def solution(mesh):
    sizes = (mesh.shape["dom"], mesh.shape["sub"])
    wide = P(None, ("dom", "sub"))
    flat = P(("dom", "sub"))
    in_specs = (wide, wide, flat, wide, wide, wide, wide, wide, flat, flat)
    return jax.shard_map(
        functools.partial(body, sizes),
        mesh=mesh,
        in_specs=in_specs,
        out_specs=wide,
        check_vma=False,
    )
```

time: 12.8 us -> 12.2 us (0.953)
  Pallas kernels: 11.9 us -> 11.2 us
    pallas_call x1, Pallas kernels: 11.9 us -> 11.2 us  [body(): pl.pallas_call(functools.partial(kernel, sizes), out_shape=pltpu.VMEM(nod...]
where the time goes in v1:
time: 12.2 us; the launch traced here: 12.1 us
  Pallas kernels  11.2 us (92%)
  local copies, waits for them, and re-layouts  0.8 us (7%)
    pallas_call x1, Pallas kernels, body(): pl.pallas_call(functools.partial(kernel, sizes), out_shape=pltpu.VMEM(nod...  11.2 us
    unnamed x1, local copies, waits for them, and re-layouts  0.8 us

profile of v1, /device:TPU:0, one launch (start us, length us, event | category | flops | bytes accessed | tf_op | source)
XLA Modules:
  0.0 12.1 jit_solution(16124110914584549680)
XLA Ops:
  0.0 11.2 %shard_map.127 = f32[512,256]{1,0:T(8,128)S(1)} custom-call(f32[512,256]{1,0:T(8,128)} %u_hbm.1, f32[512,256]{1,0:T(8,128)} %kappa_hbm.1, s32[1,256]{1,0:T(1,128)} %bitcast.2, s32[2,64]{1,0:T(2,128)} %local_hbm.1, s32[2,32]{1,0:T(2,128)} %sub_hbm.1, s32[2,32]{1,0:T(2,128)} %near_hbm.1, s32[2,12]{1,0:T(2,128)} %far_hbm.1, s32[4,3]{1,0:T(4,128)} %child_hbm.1, ...), custom_call_target="tpu_custom_call" | custom-call | tf_op jit(solution)/shard_map/pallas_call | solution.py:646
  11.3 0.8 %copy.15 = f32[512,256]{1,0:T(8,128)} copy(f32[512,256]{1,0:T(8,128)S(1)} %shard_map.127) | data formatting | bytes 1048576

commit v2 on v1

--- a/solution.py
+++ b/solution.py
@@ -142,17 +142,20 @@
     return np.concatenate(pieces, axis=0)
 
 
-def folds(krons):
-    one = np.eye(NPTS)
-    apply = np.concatenate(
-        [np.kron(one, one), np.kron(DERIV.T, one), np.kron(one, DERIV.T)], axis=1
-    )
-    heads = [np.eye(NPTS * NPTS)] * 2 + [m.T for m in krons] + krons
-    table = np.concatenate([(head @ apply).T for head in heads], axis=1)
-    return np.concatenate(numpy_halves(table), axis=0)
-
-
-def kernel(
+def folds():
+    eye = np.eye(NPTS)
+    heads = [(eye, eye)] * 2
+    heads += [(HALVES[m // 2], HALVES[m % 2]) for m in range(4)]
+    heads += [(HALVES[m // 2].T, HALVES[m % 2].T) for m in range(4)]
+    rows, tiles = [], []
+    for turn in (eye, DERIV):
+        rows.append([np.repeat(turn @ first, NPTS, axis=1) for first, _ in heads])
+        tiles.append([np.tile(turn @ second, (1, NPTS)) for _, second in heads])
+    table = [np.concatenate(kind, axis=1) for kind in rows + tiles]
+    return np.concatenate(table, axis=0).astype(np.float32)
+
+
+def steps(
     sizes,
     u_hbm,
     kappa_hbm,
@@ -160,28 +163,27 @@
     local_hbm,
     sub_hbm,
     near_hbm,
-    far_hbm,
-    child_hbm,
-    coarse_hbm,
     fold_hbm,
     deriv_hbm,
     mortar_hbm,
+    far_hbm,
+    child_hbm,
     peer_hbm,
+    coarse_hbm,
     out_ref,
     level_ref,
     local_ref,
     sub_ref,
     near_ref,
-    far_ref,
-    child_ref,
-    coarse_ref,
     fold_ref,
     deriv_ref,
     mortar_ref,
+    far_ref,
+    child_ref,
     peer_ref,
+    coarse_ref,
     w_ref,
-    u_ref,
-    k_ref,
+    uk_ref,
     g_ref,
     side_out,
     side_in,
@@ -189,16 +191,17 @@
     far_in,
     mort_out,
     mort_in,
+    side_recv,
+    far_recv,
+    mort_recv,
     small_sem,
     load_sem,
     side_send,
-    side_recv,
     far_send,
-    far_recv,
     mort_send,
-    mort_recv,
 ):
     n_dom, n_sub = sizes
+    u_ref, k_ref = uk_ref.at[0], uk_ref.at[1]
     parts = u_ref.shape[0]
     elems = parts * 128
     square = NPTS * NPTS
@@ -206,6 +209,7 @@
     me, sub = lax.axis_index("dom"), lax.axis_index("sub")
 
     urgent = [
+        (fold_hbm, fold_ref),
         (far_hbm, far_ref),
         (child_hbm, child_ref),
         (coarse_hbm, coarse_ref),
@@ -213,7 +217,6 @@
         (peer_hbm, peer_ref),
     ]
     later = [
-        (fold_hbm, fold_ref),
         (local_hbm, local_ref),
         (sub_hbm, sub_ref),
         (near_hbm, near_ref),
@@ -227,19 +230,23 @@
     block = 128
     blocks = NPTS**3 // block
 
-    def load(n, part, source, target, slot):
+    def load(n, part, source, target):
         own = pl.ds(part * block, block)
         return pltpu.make_async_copy(
-            source.at[own, pl.ds(n * 128, 128)], target.at[n, own], load_sem.at[slot, n, part]
+            source.at[own, pl.ds(n * 128, 128)], target.at[n, own], load_sem.at[part]
         )
 
-    for copy in small[:5]:
+    def loaded(part):
+        whole = uk_ref.at[0, :, pl.ds(0, 2 * block)]
+        pltpu.make_async_copy(whole, whole, load_sem.at[part]).wait()
+
+    for copy in small[:6]:
         copy.start()
     for part in range(blocks):
         for n in range(parts):
-            load(n, part, u_hbm, u_ref, 0).start()
-            load(n, part, kappa_hbm, k_ref, 1).start()
-    for copy in small[5:]:
+            load(n, part, u_hbm, u_ref).start()
+            load(n, part, kappa_hbm, k_ref).start()
+    for copy in small[6:]:
         copy.start()
 
     far_in[...] = jnp.zeros(far_in.shape, F32)
@@ -283,7 +290,6 @@
     lane = lax.broadcasted_iota(I32, (8, sources), 1)
     row8 = lax.broadcasted_iota(I32, (8, sources), 0)
     on_low = (lane < farp) | (lane >= kids_at)
-    on_low_plane = jnp.concatenate([on_low] * NPTS, axis=0)
     reach = [
         jnp.where(on_low, float(WEIGHTS[c] * DERIV[c, 0]), float(WEIGHTS[c] * DERIV[c, last]))
         for c in range(NPTS)
@@ -298,75 +304,122 @@
     for k in range(NPTS):
         quad8 = jnp.where(row8 == k, float(WEIGHTS[k]), quad8)
 
-    for copy in small[:5]:
+    for copy in small[:6]:
         copy.wait()
 
-    columns = [
-        column(far_ref[0:1], farp) - float(4 * elems),
-        column(far_ref[1:2], farp) - float(5 * elems),
-        column(coarse_ref[...], coarsep) - float(5 * elems),
-    ] + [column(child_ref[m : m + 1], groupp) - float(4 * elems) for m in range(4)]
-    columns.append(jnp.full((sources - used, 1), -1.0, F32))
-    hot_src = hot_rows(columns, 0, elems)
-
+    def held(first, ids, base):
+        total = jnp.zeros((8, sources), I32)
+        for slot, value in enumerate(ids):
+            total = jnp.where(lane == first + slot, value + (1 - base * elems), total)
+        return total
+
+    ids = held(0, [far_ref[0, c] for c in range(far)], 4)
+    ids += held(farp, [far_ref[1, c] for c in range(far)], 5)
+    ids += held(coarse_at, [coarse_ref[c] for c in range(n_dom)], 5)
+    for m in range(4):
+        ids += held(kids_at + m * groupp, [child_ref[m, c] for c in range(groups)], 4)
+    fold = []
+    for rows_kind, tile_kind in ((0, 0), (1, 0), (0, 1)):
+        tile = fold_ref[(2 + tile_kind) * NPTS : (3 + tile_kind) * NPTS, :]
+        for i in range(NPTS):
+            at = rows_kind * NPTS + i
+            fold.append(fold_ref[at : at + 1, :] * tile)
+    fold_high, fold_low = halves_of(jnp.concatenate(fold, axis=0))
+    element = lax.broadcasted_iota(I32, (elems, sources), 0) + 1
+    hot_src = jnp.where(element == ids[0:1], 1.0, 0.0).astype(BF16)
     scale = jnp.exp2(-level_ref[...].astype(F32))
     over = ((1,), (1,))
-    chosen = dot(jnp.broadcast_to(scale, (16, elems)).astype(BF16), hot_src, over)[0:8]
-    chosen = chosen * quad8
-
-    for n in range(blocks * parts):
-        load(n // blocks, n % blocks, u_hbm, u_ref, 0).wait()
-        load(n // blocks, n % blocks, kappa_hbm, k_ref, 1).wait()
-
-    def pick(ref, k):
-        own = pl.ds(k, square, NPTS)
-        high, low = halves_of(jnp.concatenate([ref[n, own, :] for n in range(parts)], axis=1))
-        return dot(high, hot_src, over) + dot(low, hot_src, over)
-
-    order = [0, last] + list(range(1, last))
-    u_of, k_of = [None] * NPTS, [None] * NPTS
-    for k in order:
-        u_of[k], k_of[k] = pick(u_ref, k), pick(k_ref, k)
-    u_plane = jnp.where(on_low_plane, u_of[0], u_of[last])
-    k_plane = jnp.where(on_low_plane, k_of[0], k_of[last])
-
-    def strip(plane, i):
-        return plane[i * NPTS : (i + 1) * NPTS]
+
+    def pick(ref, part):
+        rows = []
+        for k in range(NPTS):
+            own = pl.ds(part * block + k, block // NPTS, NPTS)
+            rows.append(jnp.concatenate([ref[n, own, :] for n in range(parts)], axis=1))
+        high, low = halves_of(jnp.concatenate(rows, axis=0))
+        both = dot(jnp.concatenate([high, low], axis=0), hot_src)
+        return both[0:block] + both[block:]
+
+    spot = jnp.bitwise_and(ids - 1, 127)
+    piece = lax.shift_right_arithmetic(ids - 1, 7)
+    lookup = lax.GatherDimensionNumbers(
+        offset_dims=(),
+        collapsed_slice_dims=(1,),
+        start_index_map=(1,),
+        operand_batching_dims=(0,),
+        start_indices_batching_dims=(0,),
+    )
+
+    def fetch(ref, part):
+        rows = []
+        for k in range(NPTS):
+            for at in range(0, block, NPTS * NPTS):
+                own = pl.ds(part * block + at + k, NPTS, NPTS)
+                tiles = []
+                for first in range(0, sources, 128):
+                    where = slice(first, first + 128)
+                    found = jnp.zeros((8, 128), F32)
+                    for n in range(parts):
+                        taken = lax.gather(
+                            ref[n, own, :],
+                            spot[:, where][..., None],
+                            lookup,
+                            slice_sizes=(1, 1),
+                            mode=lax.GatherScatterMode.PROMISE_IN_BOUNDS,
+                        )
+                        found = jnp.where(piece[:, where] == n, taken, found)
+                    tiles.append(found)
+                rows.append(tiles[0] if len(tiles) == 1 else jnp.concatenate(tiles, axis=1))
+        return jnp.concatenate(rows, axis=0)
 
     edge = float(WEIGHTS[0])
-    up_i = line([strip(u_plane, i) for i in range(NPTS)], DERIV)
-    along_k, along_i, along_j = [], [], []
-    for i in range(NPTS):
-        here = chosen * float(WEIGHTS[i])
-        g = strip(k_plane, i) * (here * edge)
-        along_i.append(up_i[i] * g)
-        flat = strip(u_plane, i)
-        turned = turn8[0] * flat
-        for r in range(1, NPTS):
-            turned += turn8[r] * pltpu.roll(flat, NPTS - r, 0)
-        along_j.append(turned * g)
-        deep = line([strip(u_of[k], i) for k in range(NPTS)], DERIV)
-        total = reach[0] * strip(k_of[0], i) * deep[0]
-        for c in range(1, NPTS):
-            total += reach[c] * strip(k_of[c], i) * deep[c]
-        along_k.append(total * here)
-    flux = jnp.concatenate(along_k + along_i + along_j, axis=0).T
-
-    small[5].wait()
-    fold = fold_ref.shape[0] // 2
+    chosen = None
+    along_k, along_j, plane_u, plane_g = [], [], [], []
+    for part in range(blocks):
+        loaded(part)
+    for part in range(blocks):
+        u_part, k_part = fetch(u_ref, part), pick(k_ref, part)
+        if chosen is None:
+            chosen = dot(jnp.broadcast_to(scale, (16, elems)).astype(BF16), hot_src)[0:8]
+            chosen = chosen * quad8
+        wide = block // NPTS
+        for i in range(part * wide // NPTS, (part + 1) * wide // NPTS):
+            at = i * NPTS - part * wide
+
+            def strip(values, k):
+                return values[k * wide + at : k * wide + at + NPTS]
+
+            here = chosen * float(WEIGHTS[i])
+            flat = jnp.where(on_low, strip(u_part, 0), strip(u_part, last))
+            g = jnp.where(on_low, strip(k_part, 0), strip(k_part, last)) * (here * edge)
+            plane_u.append(flat)
+            plane_g.append(g)
+            turned = turn8[0] * flat
+            for r in range(1, NPTS):
+                turned += turn8[r] * pltpu.roll(flat, NPTS - r, 0)
+            along_j.append(turned * g)
+            deep = line([strip(u_part, k) for k in range(NPTS)], DERIV)
+            total = reach[0] * strip(k_part, 0) * deep[0]
+            for c in range(1, NPTS):
+                total += reach[c] * strip(k_part, c) * deep[c]
+            along_k.append(total * here)
+    across_i = line(plane_u, DERIV)
+    along_i = [across_i[i] * plane_g[i] for i in range(NPTS)]
+    flux = jnp.concatenate(along_k + along_i + along_j, axis=0)
+
+    flux = flux.T
 
     def folded(rows, first, width):
         high, low = halves_of(rows)
-        cols = pl.ds(first, width)
+        cols = slice(first, first + width)
         return (
-            dot(high, fold_ref[0:fold, cols])
-            + dot(low, fold_ref[0:fold, cols])
-            + dot(high, fold_ref[fold:, cols])
+            dot(high, fold_high[:, cols])
+            + dot(low, fold_high[:, cols])
+            + dot(high, fold_low[:, cols])
         )
 
-    own = folded(flux[0:up(used, 16)], 0, 128)
+    raised = folded(flux[coarse_at:kids_at], 384, 256)
     kids = folded(flux[kids_at:used], 128, 256)
-    raised = folded(flux[coarse_at:kids_at], 384, 256)
+    own = folded(flux[0 : up(used, 16)], 0, 128)
 
     half = lax.broadcasted_iota(I32, (8, 128), 1) < square
     for side in range(2):
@@ -539,7 +592,7 @@
         hit = at == keys[0]
         for key in keys[1:]:
             hit = hit | (at == key)
-        return dot(jnp.where(hit, 1.0, 0.0).astype(BF16), hot_src).astype(BF16)
+        return dot(jnp.where(hit, 1.0, 0.0).astype(BF16), hot_src, over).astype(BF16)
 
     src = lax.broadcasted_iota(I32, (1, sources), 1)
 
@@ -567,8 +620,11 @@
     for m in range(4):
         first = kids_at + m * groupp
         share.append(product(joined, lift[m]) - own[first : first + groupp, 0:square])
-    hot_kids = hot_src[kids_at:used]
-    add_across(low_k, spread_rows(jnp.concatenate(share, axis=0), hot_kids))
+    share = [jnp.zeros((kids_at, square), F32)] + share
+    if sources > used:
+        share.append(jnp.zeros((sources - used, square), F32))
+    high, low = halves_of(jnp.concatenate(share, axis=0).T)
+    add_across(low_k, dot(high, hot_src, over) + dot(low, hot_src, over))
     add_across(low_i, spread_rows(take_rows(hot1l, face1), hot0l))
     add_across(high_i, spread_rows(take_rows(hot0l, face0), hot1l))
 
@@ -585,16 +641,22 @@
         add_across(slab(i, 0), add2[i * NPTS : (i + 1) * NPTS])
         add_across(slab(i, last), add3[i * NPTS : (i + 1) * NPTS])
 
-    def wait_all(step, carry):
-        mail(step, True).wait()
+    def sent_all(step, carry):
+        mail(step, True).wait_send()
         return carry
 
-    lax.fori_loop(1, n_dom, wait_all, 0, unroll=n_dom <= 8)
+    lax.fori_loop(1, n_dom, sent_all, 0, unroll=n_dom <= 8)
     for side in range(2):
         for s in range(shifts):
             @pl.when(far_there(side, s))
             def _():
                 far_copy(side, s, True).wait()
+
+    def wait_all(step, carry):
+        mail(step, True).wait_recv()
+        return carry
+
+    lax.fori_loop(1, n_dom, wait_all, 0, unroll=n_dom <= 8)
 
     received = [far_in[0], far_in[1], mort_in[...]]
     spare = keyed - 2 * farp - 8 * n_dom
@@ -607,6 +669,19 @@
     add_across(high_k, dot(high, land5) + dot(low, land5))
     for n in range(parts):
         out_ref[:, n * 128 : (n + 1) * 128] = w_ref[n]
+
+
+def kernel(sizes, copies, *refs):
+    n_dom, _ = sizes
+    far_recv = refs[-2]
+    pl.run_scoped(
+        functools.partial(steps, sizes, *refs),
+        pltpu.SemaphoreType.DMA((copies,)),
+        pltpu.SemaphoreType.DMA((NPTS**3 // 128,)),
+        pltpu.SemaphoreType.DMA((4,)),
+        pltpu.SemaphoreType.DMA(far_recv.shape),
+        pltpu.SemaphoreType.DMA((n_dom,)),
+    )
 
 
 def body(
@@ -634,26 +709,23 @@
         local_faces,
         sub_faces,
         near_faces,
-        far_faces,
-        child_faces,
-        coarse_faces.reshape(1, n_dom),
-        jnp.asarray(folds(krons), BF16),
+        jnp.asarray(folds(), F32),
         jnp.asarray(stencils(), BF16),
         jnp.asarray(mortar, F32),
     ]
+    tables = [far_faces, child_faces, child_peer, coarse_faces]
     hbm = pl.BlockSpec(memory_space=pltpu.HBM)
     vmem = pl.BlockSpec(memory_space=pltpu.VMEM)
     return pl.pallas_call(
-        functools.partial(kernel, sizes),
+        functools.partial(kernel, sizes, len(small) + len(tables)),
         out_shape=pltpu.VMEM(nodal_values.shape, F32),
         in_specs=[hbm] * 13,
         out_specs=vmem,
         scratch_shapes=[pltpu.VMEM(item.shape, item.dtype) for item in small]
+        + [pltpu.SMEM(item.shape, I32) for item in tables]
         + [
-            pltpu.SMEM(child_peer.shape, I32),
             pltpu.VMEM(held, F32),
-            pltpu.VMEM(held, F32),
-            pltpu.VMEM(held, F32),
+            pltpu.VMEM((2, *held), F32),
             pltpu.VMEM(held, F32),
             pltpu.VMEM((4, side_rows, 128), F32),
             pltpu.VMEM((4, side_rows, 128), F32),
@@ -661,13 +733,8 @@
             pltpu.VMEM((2, far_rows, 128), F32),
             pltpu.VMEM((n_dom * 8, 128), F32),
             pltpu.VMEM((n_dom * 8, 128), F32),
-            pltpu.SemaphoreType.DMA((len(small) + 1,)),
-            pltpu.SemaphoreType.DMA((2, held[0], NPTS**3 // 128)),
-            pltpu.SemaphoreType.DMA((4,)),
             pltpu.SemaphoreType.DMA((4,)),
             pltpu.SemaphoreType.DMA((2, far_faces.shape[1] // FAR)),
-            pltpu.SemaphoreType.DMA((2, far_faces.shape[1] // FAR)),
-            pltpu.SemaphoreType.DMA((n_dom,)),
             pltpu.SemaphoreType.DMA((n_dom,)),
         ],
         compiler_params=pltpu.CompilerParams(
@@ -677,7 +744,7 @@
         nodal_values,
         kappa,
         *small,
-        child_peer,
+        *tables,
     )
 
 

time: 12.2 us -> 11.3 us (0.926)
  Pallas kernels: 11.2 us -> 10.4 us
    pallas_call x1, Pallas kernels: 11.2 us -> 10.4 us  [body(): pl.pallas_call(functools.partial(kernel, sizes, len(small) + len(tables))...]
where the time goes in v2:
time: 11.3 us; the launch traced here: 11.2 us
  Pallas kernels  10.4 us (92%)
  local copies, waits for them, and re-layouts  0.8 us (7%)
    pallas_call x1, Pallas kernels, body(): pl.pallas_call(functools.partial(kernel, sizes, len(small) + len(tables))...  10.4 us
    unnamed x1, local copies, waits for them, and re-layouts  0.8 us

profile of v2, /device:TPU:0, one launch (start us, length us, event | category | flops | bytes accessed | tf_op | source)
XLA Modules:
  0.0 11.2 jit_solution(12182239871472233651)
XLA Ops:
  0.0 10.4 %shard_map.127 = f32[512,256]{1,0:T(8,128)S(1)} custom-call(f32[512,256]{1,0:T(8,128)} %refs_0_.1, f32[512,256]{1,0:T(8,128)} %refs_1_.1, s32[1,256]{1,0:T(1,128)} %bitcast.1, s32[2,64]{1,0:T(2,128)} %refs_3_.1, s32[2,32]{1,0:T(2,128)} %refs_4_.1, s32[2,32]{1,0:T(2,128)} %refs_5_.1, f32[32,640]{1,0:T(8,128)} %constant.6.clone.refs_6_, ...), custom_call_target="tpu_custom_call" | custom-call | tf_op jit(solution)/shard_map/pallas_call | solution.py:719
  10.4 0.8 %copy.15 = f32[512,256]{1,0:T(8,128)} copy(f32[512,256]{1,0:T(8,128)S(1)} %shard_map.127) | data formatting | bytes 1048576

commit v3 on v2

--- a/solution.py
+++ b/solution.py
@@ -411,13 +411,10 @@
     def folded(rows, first, width):
         high, low = halves_of(rows)
         cols = slice(first, first + width)
-        return (
-            dot(high, fold_high[:, cols])
-            + dot(low, fold_high[:, cols])
-            + dot(high, fold_low[:, cols])
-        )
-
-    raised = folded(flux[coarse_at:kids_at], 384, 256)
+        both = dot(jnp.concatenate([high, low], axis=0), fold_high[:, cols])
+        return both[0 : rows.shape[0]] + both[rows.shape[0] :] + dot(high, fold_low[:, cols])
+
+    raised = folded(flux[coarse_at : coarse_at + up(coarsep, 16)], 384, 256)
     kids = folded(flux[kids_at:used], 128, 256)
     own = folded(flux[0 : up(used, 16)], 0, 128)
 
@@ -484,7 +481,9 @@
                 def _():
                     far_copy(side, s, False).start()
 
-    @pl.when(me > 0)
+    early = me < 3
+
+    @pl.when(jnp.logical_not(early))
     def _():
         send_messages()
 
@@ -559,7 +558,7 @@
     side_out[2, 0:near, 0:square] = take_rows(hot2, face2)[0:near]
     side_out[3, 0:near, 0:square] = take_rows(hot3, face3)[0:near]
 
-    @pl.when(me == 0)
+    @pl.when(early)
     def _():
         send_messages()
 

time: 11.3 us -> 11 us (0.973)
  Pallas kernels: 10.4 us -> 10 us
    pallas_call x1, Pallas kernels: 10.4 us -> 10 us  [body(): pl.pallas_call(functools.partial(kernel, sizes, len(small) + len(tables))...]
where the time goes in v3:
time: 11 us; the launch traced here: 10.9 us
  Pallas kernels  10 us (91%)
  local copies, waits for them, and re-layouts  0.8 us (7%)
    pallas_call x1, Pallas kernels, body(): pl.pallas_call(functools.partial(kernel, sizes, len(small) + len(tables))...  10 us
    unnamed x1, local copies, waits for them, and re-layouts  0.8 us

profile of v3, /device:TPU:0, one launch (start us, length us, event | category | flops | bytes accessed | tf_op | source)
XLA Modules:
  0.0 10.9 jit_solution(4252115199245138236)
XLA Ops:
  0.0 10.0 %shard_map.127 = f32[512,256]{1,0:T(8,128)S(1)} custom-call(f32[512,256]{1,0:T(8,128)} %refs_0_.1, f32[512,256]{1,0:T(8,128)} %refs_1_.1, s32[1,256]{1,0:T(1,128)} %bitcast.1, s32[2,64]{1,0:T(2,128)} %refs_3_.1, s32[2,32]{1,0:T(2,128)} %refs_4_.1, s32[2,32]{1,0:T(2,128)} %refs_5_.1, f32[32,640]{1,0:T(8,128)} %constant.6.clone.refs_6_, ...), custom_call_target="tpu_custom_call" | custom-call | tf_op jit(solution)/shard_map/pallas_call | solution.py:718
  10.1 0.8 %copy.15 = f32[512,256]{1,0:T(8,128)} copy(f32[512,256]{1,0:T(8,128)S(1)} %shard_map.127) | data formatting | bytes 1048576

commit v4 on v3

--- a/solution.py
+++ b/solution.py
@@ -170,7 +170,7 @@
     child_hbm,
     peer_hbm,
     coarse_hbm,
-    out_ref,
+    w_ref,
     level_ref,
     local_ref,
     sub_ref,
@@ -182,7 +182,6 @@
     child_ref,
     peer_ref,
     coarse_ref,
-    w_ref,
     uk_ref,
     g_ref,
     side_out,
@@ -191,14 +190,14 @@
     far_in,
     mort_out,
     mort_in,
-    side_recv,
-    far_recv,
-    mort_recv,
     small_sem,
     load_sem,
     side_send,
+    side_recv,
     far_send,
+    far_recv,
     mort_send,
+    mort_recv,
 ):
     n_dom, n_sub = sizes
     u_ref, k_ref = uk_ref.at[0], uk_ref.at[1]
@@ -509,9 +508,29 @@
     def across(ref, own):
         return jnp.concatenate([ref[n, own, :] for n in range(parts)], axis=1)
 
-    def add_across(own, values):
+    def spot_of(n, i, j):
+        return pl.ds(((i * NPTS + j) * parts + n) * NPTS, NPTS)
+
+    def face_of(tiles):
+        return jnp.concatenate(
+            [
+                jnp.concatenate([w_ref[spot_of(n, i, j), :] for i, j in tiles], axis=0)
+                for n in range(parts)
+            ],
+            axis=1,
+        )
+
+    def add_tiles(tiles, values):
+        for t, (i, j) in enumerate(tiles):
+            for n in range(parts):
+                w_ref[spot_of(n, i, j), :] += values[
+                    t * NPTS : (t + 1) * NPTS, n * 128 : (n + 1) * 128
+                ]
+
+    def add_level(k, values):
         for n in range(parts):
-            w_ref[n, own, :] += values[:, n * 128 : (n + 1) * 128]
+            own_rows = pl.ds(n * NPTS + k, square, parts * NPTS)
+            w_ref[own_rows, :] += values[:, n * 128 : (n + 1) * 128]
 
     turns = [deriv_ref[128 * n : 128 * n + 128, :] for n in range(4)]
 
@@ -531,28 +550,29 @@
         own_rows = pl.ds(part * block, block)
         turn = along(turns[0:2], across(u_ref, own_rows)) * across(g_ref, own_rows)
         turn = along(turns[2:4], turn)
-        for n in range(parts):
-            w_ref[n, own_rows, :] = turn[:, n * 128 : (n + 1) * 128]
+        for t in range(block // NPTS):
+            i, j = divmod(part * block // NPTS + t, NPTS)
+            for n in range(parts):
+                w_ref[spot_of(n, i, j), :] = turn[
+                    t * NPTS : (t + 1) * NPTS, n * 128 : (n + 1) * 128
+                ]
     for n in range(parts):
         for j in range(NPTS):
             turn = line([u_ref[n, slab(i, j), :] for i in range(NPTS)], DERIV)
             turn = [turn[i] * g_ref[n, slab(i, j), :] for i in range(NPTS)]
             turn = line(turn, DERIV.T)
             for i in range(NPTS):
-                w_ref[n, slab(i, j), :] += turn[i]
+                w_ref[spot_of(n, i, j), :] += turn[i]
         for i in range(NPTS):
             turn = line([u_ref[n, slab(i, j), :] for j in range(NPTS)], DERIV)
             turn = [turn[j] * g_ref[n, slab(i, j), :] for j in range(NPTS)]
             turn = line(turn, DERIV.T)
             for j in range(NPTS):
-                w_ref[n, slab(i, j), :] += turn[j]
-
-    low_i, high_i = pl.ds(0, square), pl.ds(last * square, square)
-    low_k, high_k = pl.ds(0, square, NPTS), pl.ds(last, square, NPTS)
-    face0 = across(w_ref, low_i)
-    face1 = across(w_ref, high_i)
-    face2 = jnp.concatenate([across(w_ref, slab(i, 0)) for i in range(NPTS)], axis=0)
-    face3 = jnp.concatenate([across(w_ref, slab(i, last)) for i in range(NPTS)], axis=0)
+                w_ref[spot_of(n, i, j), :] += turn[j]
+
+    low_i, high_i = ([(i, j) for j in range(NPTS)] for i in (0, last))
+    low_j, high_j = ([(i, j) for i in range(NPTS)] for j in (0, last))
+    face0, face1, face2, face3 = (face_of(tiles) for tiles in (low_i, high_i, low_j, high_j))
     side_out[0, 0:rim, 0:square] = take_rows(hot0s, face0)[0:rim]
     side_out[1, 0:rim, 0:square] = take_rows(hot1s, face1)[0:rim]
     side_out[2, 0:near, 0:square] = take_rows(hot2, face2)[0:near]
@@ -623,22 +643,21 @@
     if sources > used:
         share.append(jnp.zeros((sources - used, square), F32))
     high, low = halves_of(jnp.concatenate(share, axis=0).T)
-    add_across(low_k, dot(high, hot_src, over) + dot(low, hot_src, over))
-    add_across(low_i, spread_rows(take_rows(hot1l, face1), hot0l))
-    add_across(high_i, spread_rows(take_rows(hot0l, face0), hot1l))
+    add_level(0, dot(high, hot_src, over) + dot(low, hot_src, over))
+    add_tiles(low_i, spread_rows(take_rows(hot1l, face1), hot0l))
+    add_tiles(high_i, spread_rows(take_rows(hot0l, face0), hot1l))
 
     for there, mine, theirs, device in sides:
         @pl.when(there)
         def _():
             side_copy(mine, mine, device).wait()
 
-    add_across(low_i, spread_rows(side_in[0, 0:rim, 0:square], hot0s))
-    add_across(high_i, spread_rows(side_in[1, 0:rim, 0:square], hot1s))
+    add_tiles(low_i, spread_rows(side_in[0, 0:rim, 0:square], hot0s))
+    add_tiles(high_i, spread_rows(side_in[1, 0:rim, 0:square], hot1s))
     add2 = spread_rows(side_in[2, 0:near, 0:square], hot2)
     add3 = spread_rows(side_in[3, 0:near, 0:square], hot3)
-    for i in range(NPTS):
-        add_across(slab(i, 0), add2[i * NPTS : (i + 1) * NPTS])
-        add_across(slab(i, last), add3[i * NPTS : (i + 1) * NPTS])
+    add_tiles(low_j, add2)
+    add_tiles(high_j, add3)
 
     def sent_all(step, carry):
         mail(step, True).wait_send()
@@ -663,23 +682,16 @@
         received.append(jnp.zeros((spare, 128), F32))
     received = jnp.concatenate(received, axis=0).T
     received = jnp.concatenate([received[0:square], received[square:]], axis=1)
-    high, low = halves_of(received)
-    add_across(low_k, dot(high, land4) + dot(low, land4))
-    add_across(high_k, dot(high, land5) + dot(low, land5))
-    for n in range(parts):
-        out_ref[:, n * 128 : (n + 1) * 128] = w_ref[n]
-
-
-def kernel(sizes, copies, *refs):
-    n_dom, _ = sizes
-    far_recv = refs[-2]
+    both = jnp.concatenate(halves_of(received), axis=0)
+    for k, land in ((0, land4), (last, land5)):
+        added = dot(both, land)
+        add_level(k, added[0:square] + added[square:])
+
+
+def kernel(sizes, semaphores, *refs):
     pl.run_scoped(
         functools.partial(steps, sizes, *refs),
-        pltpu.SemaphoreType.DMA((copies,)),
-        pltpu.SemaphoreType.DMA((NPTS**3 // 128,)),
-        pltpu.SemaphoreType.DMA((4,)),
-        pltpu.SemaphoreType.DMA(far_recv.shape),
-        pltpu.SemaphoreType.DMA((n_dom,)),
+        *[pltpu.SemaphoreType.DMA(shape) for shape in semaphores],
     )
 
 
@@ -713,17 +725,19 @@
         jnp.asarray(mortar, F32),
     ]
     tables = [far_faces, child_faces, child_peer, coarse_faces]
+    far_slots = (2, far_faces.shape[1] // FAR)
+    semaphores = [(len(small) + len(tables),), (NPTS**3 // 128,), (4,), (4,)]
+    semaphores += [far_slots, far_slots, (n_dom,), (n_dom,)]
     hbm = pl.BlockSpec(memory_space=pltpu.HBM)
     vmem = pl.BlockSpec(memory_space=pltpu.VMEM)
-    return pl.pallas_call(
-        functools.partial(kernel, sizes, len(small) + len(tables)),
-        out_shape=pltpu.VMEM(nodal_values.shape, F32),
+    applied = pl.pallas_call(
+        functools.partial(kernel, sizes, semaphores),
+        out_shape=pltpu.VMEM((held[0] * held[1], 128), F32),
         in_specs=[hbm] * 13,
         out_specs=vmem,
         scratch_shapes=[pltpu.VMEM(item.shape, item.dtype) for item in small]
         + [pltpu.SMEM(item.shape, I32) for item in tables]
         + [
-            pltpu.VMEM(held, F32),
             pltpu.VMEM((2, *held), F32),
             pltpu.VMEM(held, F32),
             pltpu.VMEM((4, side_rows, 128), F32),
@@ -732,9 +746,6 @@
             pltpu.VMEM((2, far_rows, 128), F32),
             pltpu.VMEM((n_dom * 8, 128), F32),
             pltpu.VMEM((n_dom * 8, 128), F32),
-            pltpu.SemaphoreType.DMA((4,)),
-            pltpu.SemaphoreType.DMA((2, far_faces.shape[1] // FAR)),
-            pltpu.SemaphoreType.DMA((n_dom,)),
         ],
         compiler_params=pltpu.CompilerParams(
             collective_id=0, has_side_effects=True, vmem_limit_bytes=60 * 1024 * 1024
@@ -745,6 +756,8 @@
         *small,
         *tables,
     )
+    applied = applied.reshape(NPTS * NPTS, held[0], NPTS, 128).transpose(0, 2, 1, 3)
+    return applied.reshape(nodal_values.shape)
 
 
 def solution(mesh):

time: 11 us -> 10.8 us (0.982)
  Pallas kernels: 10 us -> 9.85 us
    pallas_call x1, Pallas kernels: 10 us -> 9.85 us  [body(): pl.pallas_call(functools.partial(kernel, sizes, semaphores), out_shape=pl...]
where the time goes in v4:
time: 10.8 us; the launch traced here: 10.7 us
  Pallas kernels  9.85 us (91%)
  local copies, waits for them, and re-layouts  0.8 us (7%)
    pallas_call x1, Pallas kernels, body(): pl.pallas_call(functools.partial(kernel, sizes, semaphores), out_shape=pl...  9.85 us
    unnamed x1, local copies, waits for them, and re-layouts  0.8 us

profile of v4, /device:TPU:0, one launch (start us, length us, event | category | flops | bytes accessed | tf_op | source)
XLA Modules:
  0.0 10.7 jit_solution(12300230901567419488)
XLA Ops:
  0.0 9.9 %shard_map.127 = f32[1024,128]{1,0:T(8,128)S(1)} custom-call(f32[512,256]{1,0:T(8,128)} %refs_0_.1, f32[512,256]{1,0:T(8,128)} %refs_1_.1, s32[1,256]{1,0:T(1,128)} %bitcast.7, s32[2,64]{1,0:T(2,128)} %refs_3_.1, s32[2,32]{1,0:T(2,128)} %refs_4_.1, s32[2,32]{1,0:T(2,128)} %refs_5_.1, f32[32,640]{1,0:T(8,128)} %constant.6.clone.refs_6_, ...), custom_call_target="tpu_custom_call" | custom-call | tf_op jit(solution)/shard_map/pallas_call | solution.py:733
  9.9 0.8 %copy.15 = f32[512,256]{1,0:T(8,128)} copy(f32[512,256]{1,0:T(8,128)S(1)} %bitcast.6) | data formatting | bytes 1048576

commit v5 on v4

--- a/solution.py
+++ b/solution.py
@@ -143,16 +143,11 @@
 
 
 def folds():
-    eye = np.eye(NPTS)
-    heads = [(eye, eye)] * 2
-    heads += [(HALVES[m // 2], HALVES[m % 2]) for m in range(4)]
-    heads += [(HALVES[m // 2].T, HALVES[m % 2].T) for m in range(4)]
-    rows, tiles = [], []
-    for turn in (eye, DERIV):
-        rows.append([np.repeat(turn @ first, NPTS, axis=1) for first, _ in heads])
-        tiles.append([np.tile(turn @ second, (1, NPTS)) for _, second in heads])
-    table = [np.concatenate(kind, axis=1) for kind in rows + tiles]
-    return np.concatenate(table, axis=0).astype(np.float32)
+    heads = [(HALVES[m // 2], HALVES[m % 2]) for m in range(4)]
+    heads += [(first.T, second.T) for first, second in heads]
+    rows = np.concatenate([np.repeat(first, NPTS, axis=1) for first, _ in heads], axis=1)
+    tiles = np.concatenate([np.tile(second, (1, NPTS)) for _, second in heads], axis=1)
+    return np.concatenate([rows, tiles], axis=0).astype(np.float32)
 
 
 def steps(
@@ -293,12 +288,23 @@
         jnp.where(on_low, float(WEIGHTS[c] * DERIV[c, 0]), float(WEIGHTS[c] * DERIV[c, last]))
         for c in range(NPTS)
     ]
-    turn8 = []
-    for r in range(NPTS):
-        table = jnp.zeros((8, sources), F32)
-        for b in range(NPTS):
-            table = jnp.where(row8 == b, float(DERIV[b, (b + r) % NPTS]), table)
-        turn8.append(table)
+
+    def shifted(matrix):
+        tables = []
+        for r in range(NPTS):
+            table = jnp.zeros((8, sources), F32)
+            for b in range(NPTS):
+                table = jnp.where(row8 == b, float(matrix[b, (b + r) % NPTS]), table)
+            tables.append(table)
+        return tables
+
+    def turn(tables, values):
+        total = tables[0] * values
+        for r in range(1, NPTS):
+            total += tables[r] * pltpu.roll(values, NPTS - r, 0)
+        return total
+
+    forth8, back8 = shifted(DERIV), shifted(DERIV.T)
     quad8 = jnp.zeros((8, sources), F32)
     for k in range(NPTS):
         quad8 = jnp.where(row8 == k, float(WEIGHTS[k]), quad8)
@@ -317,13 +323,6 @@
     ids += held(coarse_at, [coarse_ref[c] for c in range(n_dom)], 5)
     for m in range(4):
         ids += held(kids_at + m * groupp, [child_ref[m, c] for c in range(groups)], 4)
-    fold = []
-    for rows_kind, tile_kind in ((0, 0), (1, 0), (0, 1)):
-        tile = fold_ref[(2 + tile_kind) * NPTS : (3 + tile_kind) * NPTS, :]
-        for i in range(NPTS):
-            at = rows_kind * NPTS + i
-            fold.append(fold_ref[at : at + 1, :] * tile)
-    fold_high, fold_low = halves_of(jnp.concatenate(fold, axis=0))
     element = lax.broadcasted_iota(I32, (elems, sources), 0) + 1
     hot_src = jnp.where(element == ids[0:1], 1.0, 0.0).astype(BF16)
     scale = jnp.exp2(-level_ref[...].astype(F32))
@@ -374,8 +373,9 @@
     chosen = None
     along_k, along_j, plane_u, plane_g = [], [], [], []
     for part in range(blocks):
-        loaded(part)
-    for part in range(blocks):
+        if part % 2 == 0:
+            loaded(part)
+            loaded(part + 1)
         u_part, k_part = fetch(u_ref, part), pick(k_ref, part)
         if chosen is None:
             chosen = dot(jnp.broadcast_to(scale, (16, elems)).astype(BF16), hot_src)[0:8]
@@ -392,20 +392,20 @@
             g = jnp.where(on_low, strip(k_part, 0), strip(k_part, last)) * (here * edge)
             plane_u.append(flat)
             plane_g.append(g)
-            turned = turn8[0] * flat
-            for r in range(1, NPTS):
-                turned += turn8[r] * pltpu.roll(flat, NPTS - r, 0)
-            along_j.append(turned * g)
+            along_j.append(turn(back8, turn(forth8, flat) * g))
             deep = line([strip(u_part, k) for k in range(NPTS)], DERIV)
             total = reach[0] * strip(k_part, 0) * deep[0]
             for c in range(1, NPTS):
                 total += reach[c] * strip(k_part, c) * deep[c]
             along_k.append(total * here)
+    fold = [
+        fold_ref[i : i + 1, :] * fold_ref[NPTS : 2 * NPTS, :] for i in range(NPTS)
+    ]
+    fold_high, fold_low = halves_of(jnp.concatenate(fold, axis=0))
     across_i = line(plane_u, DERIV)
-    along_i = [across_i[i] * plane_g[i] for i in range(NPTS)]
-    flux = jnp.concatenate(along_k + along_i + along_j, axis=0)
-
-    flux = flux.T
+    along_i = line([across_i[i] * plane_g[i] for i in range(NPTS)], DERIV.T)
+    summed = [along_i[i] + (along_j[i] + along_k[i]) for i in range(NPTS)]
+    own = jnp.concatenate(summed + summed, axis=0).T
 
     def folded(rows, first, width):
         high, low = halves_of(rows)
@@ -413,9 +413,8 @@
         both = dot(jnp.concatenate([high, low], axis=0), fold_high[:, cols])
         return both[0 : rows.shape[0]] + both[rows.shape[0] :] + dot(high, fold_low[:, cols])
 
-    raised = folded(flux[coarse_at : coarse_at + up(coarsep, 16)], 384, 256)
-    kids = folded(flux[kids_at:used], 128, 256)
-    own = folded(flux[0 : up(used, 16)], 0, 128)
+    raised = folded(own[coarse_at : coarse_at + up(coarsep, 16), 0:square], 256, 256)
+    kids = folded(own[kids_at:used, 0:square], 0, 256)
 
     half = lax.broadcasted_iota(I32, (8, 128), 1) < square
     for side in range(2):

time: 10.8 us -> 10.6 us (0.981)
  Pallas kernels: 9.85 us -> 9.68 us
    pallas_call x1, Pallas kernels: 9.85 us -> 9.68 us  [body(): pl.pallas_call(functools.partial(kernel, sizes, semaphores), out_shape=pl...]
where the time goes in v5:
time: 10.6 us; the launch traced here: 10.5 us
  Pallas kernels  9.68 us (91%)
  local copies, waits for them, and re-layouts  0.8 us (8%)
    pallas_call x1, Pallas kernels, body(): pl.pallas_call(functools.partial(kernel, sizes, semaphores), out_shape=pl...  9.68 us
    unnamed x1, local copies, waits for them, and re-layouts  0.8 us

profile of v5, /device:TPU:0, one launch (start us, length us, event | category | flops | bytes accessed | tf_op | source)
XLA Modules:
  0.0 10.5 jit_solution(14458013746125407046)
XLA Ops:
  0.0 9.7 %shard_map.127 = f32[1024,128]{1,0:T(8,128)S(1)} custom-call(f32[512,256]{1,0:T(8,128)} %refs_0_.1, f32[512,256]{1,0:T(8,128)} %refs_1_.1, s32[1,256]{1,0:T(1,128)} %bitcast.7, s32[2,64]{1,0:T(2,128)} %refs_3_.1, s32[2,32]{1,0:T(2,128)} %refs_4_.1, s32[2,32]{1,0:T(2,128)} %refs_5_.1, f32[16,512]{1,0:T(8,128)} %constant.6.clone.refs_6_, ...), custom_call_target="tpu_custom_call" | custom-call | tf_op jit(solution)/shard_map/pallas_call | solution.py:732
  9.7 0.8 %copy.15 = f32[512,256]{1,0:T(8,128)} copy(f32[512,256]{1,0:T(8,128)S(1)} %bitcast.6) | data formatting | bytes 1048576

commit v6 on v5

--- a/solution.py
+++ b/solution.py
@@ -166,6 +166,8 @@
     peer_hbm,
     coarse_hbm,
     w_ref,
+    arrived_ref,
+    land_ref,
     level_ref,
     local_ref,
     sub_ref,
@@ -629,8 +631,8 @@
     p = src - coarse_at
     holds = (p >= 0) & (p < n_dom)
     key5 = jnp.where(holds, 2 * farp + 8 * p, key5)
-    land4 = landing_rows([key4])
-    land5 = landing_rows([key5, jnp.where(holds, keyed + 2 * farp + 8 * p, -1)])
+    land_ref[0] = landing_rows([key4])
+    land_ref[1] = landing_rows([key5, jnp.where(holds, keyed + 2 * farp + 8 * p, -1)])
 
     joined = projected[:, 0:square] + projected[:, square:]
     lift = [mortar_ref[m * square : (m + 1) * square, :] for m in range(4)]
@@ -675,16 +677,9 @@
 
     lax.fori_loop(1, n_dom, wait_all, 0, unroll=n_dom <= 8)
 
-    received = [far_in[0], far_in[1], mort_in[...]]
-    spare = keyed - 2 * farp - 8 * n_dom
-    if spare:
-        received.append(jnp.zeros((spare, 128), F32))
-    received = jnp.concatenate(received, axis=0).T
-    received = jnp.concatenate([received[0:square], received[square:]], axis=1)
-    both = jnp.concatenate(halves_of(received), axis=0)
-    for k, land in ((0, land4), (last, land5)):
-        added = dot(both, land)
-        add_level(k, added[0:square] + added[square:])
+    arrived_ref[0:farp] = far_in[0]
+    arrived_ref[farp : 2 * farp] = far_in[1]
+    arrived_ref[2 * farp :] = mort_in[...]
 
 
 def kernel(sizes, semaphores, *refs):
@@ -692,6 +687,43 @@
         functools.partial(steps, sizes, *refs),
         *[pltpu.SemaphoreType.DMA(shape) for shape in semaphores],
     )
+
+
+def finish(w_ref, arrived_ref, land_ref, out_hbm, ends_ref):
+    def run(sem):
+        square = NPTS * NPTS
+        tiles, parts = w_ref.shape[0] // NPTS, w_ref.shape[0] // NPTS // square
+        inner = pltpu.make_async_copy(
+            w_ref.reshape(tiles, NPTS, 128).at[:, 1 : NPTS - 1],
+            out_hbm.reshape(tiles, NPTS, 128).at[:, 1 : NPTS - 1],
+            sem.at[2 * parts],
+        )
+        inner.start()
+        received = arrived_ref[...]
+        spare = land_ref.shape[1] // 2 - received.shape[0]
+        if spare:
+            received = jnp.concatenate([received, jnp.zeros((spare, 128), F32)], axis=0)
+        received = received.T
+        received = jnp.concatenate([received[0:square], received[square:]], axis=1)
+        both = jnp.concatenate(halves_of(received), axis=0)
+        rim = out_hbm.reshape(square, parts, NPTS, 128)
+        copies = [inner]
+        for side, k in enumerate((0, NPTS - 1)):
+            added = dot(both, land_ref[side])
+            added = added[0:square] + added[square:]
+            for n in range(parts):
+                rows = w_ref[pl.ds(n * NPTS + k, square, parts * NPTS), :]
+                ends_ref[side, n] = rows + added[:, n * 128 : (n + 1) * 128]
+                copy = pltpu.make_async_copy(
+                    ends_ref.at[side, n], rim.at[:, n, k], sem.at[side * parts + n]
+                )
+                copies.append(copy)
+        for copy in copies[1:]:
+            copy.start()
+        for copy in copies:
+            copy.wait()
+
+    pl.run_scoped(run, pltpu.SemaphoreType.DMA((2 * w_ref.shape[0] // NPTS**3 + 1,)))
 
 
 def body(
@@ -729,11 +761,16 @@
     semaphores += [far_slots, far_slots, (n_dom,), (n_dom,)]
     hbm = pl.BlockSpec(memory_space=pltpu.HBM)
     vmem = pl.BlockSpec(memory_space=pltpu.VMEM)
-    applied = pl.pallas_call(
+    arrivals = 2 * far_rows + 8 * n_dom
+    parts = pl.pallas_call(
         functools.partial(kernel, sizes, semaphores),
-        out_shape=pltpu.VMEM((held[0] * held[1], 128), F32),
+        out_shape=[
+            pltpu.VMEM((held[0] * held[1], 128), F32),
+            pltpu.VMEM((arrivals, 128), F32),
+            pltpu.VMEM((2, 2 * up(arrivals, 128), elems), BF16),
+        ],
         in_specs=[hbm] * 13,
-        out_specs=vmem,
+        out_specs=[vmem] * 3,
         scratch_shapes=[pltpu.VMEM(item.shape, item.dtype) for item in small]
         + [pltpu.SMEM(item.shape, I32) for item in tables]
         + [
@@ -755,6 +792,13 @@
         *small,
         *tables,
     )
+    applied = pl.pallas_call(
+        finish,
+        out_shape=jax.ShapeDtypeStruct((held[0] * held[1], 128), F32),
+        in_specs=[vmem] * 3,
+        out_specs=hbm,
+        scratch_shapes=[pltpu.VMEM((2, held[0], NPTS * NPTS, 128), F32)],
+    )(*[pltpu.with_memory_space_constraint(item, pltpu.VMEM) for item in parts])
     applied = applied.reshape(NPTS * NPTS, held[0], NPTS, 128).transpose(0, 2, 1, 3)
     return applied.reshape(nodal_values.shape)
 

time: 10.6 us -> 10.5 us (level)
  local copies, waits for them, and re-layouts: 0.8 us -> 0 us
  Pallas kernels: 9.68 us -> 10.3 us
    unnamed x1 -> x0, local copies, waits for them, and re-layouts: 0.8 us -> none
    pallas_call x1 -> x2, Pallas kernels: 9.68 us -> 10.3 us  [the longest x1 9.42 us: body(): pl.pallas_call(functools.partial(kernel, sizes, semaphores), out_shape=[p...]
where the time goes in v6:
time: 10.5 us; the launch traced here: 10.3 us
  Pallas kernels  10.3 us (98%)
    pallas_call x1, Pallas kernels, body(): pl.pallas_call(functools.partial(kernel, sizes, semaphores), out_shape=[p...  9.42 us
    pallas_call x1, Pallas kernels, body(): pl.pallas_call(finish, out_shape=jax.ShapeDtypeStruct((held[0] * held[1],...  0.89 us

profile of v6, /device:TPU:0, one launch (start us, length us, event | category | flops | bytes accessed | tf_op | source)
XLA Modules:
  0.0 10.3 jit_solution(9105235176509354731)
XLA Ops:
  0.0 9.4 %shard_map.127 = (f32[1024,128]{1,0:T(8,128)S(1)}, f32[96,128]{1,0:T(8,128)S(1)}, bf16[2,256,256]{2,1,0:T(8,128)(2,1)S(1)}) custom-call(f32[512,256]{1,0:T(8,128)} %refs_0_.1, f32[512,256]{1,0:T(8,128)} %refs_1_.1, s32[1,256]{1,0:T(1,128)} %bitcast.6, s32[2,64]{1,0:T(2,128)} %refs_3_.1, s32[2,32]{1,0:T(2,128)} %refs_4_.1, s32[2,32]{1,0:T(2,128)} %refs_5_.1, ...), custom_call_target="tpu_custom_call" | custom-call | tf_op jit(solution)/shard_map/pallas_call | solution.py:765
  9.4 0.9 %shard_map.128 = f32[1024,128]{1,0:T(8,128)} custom-call(f32[1024,128]{1,0:T(8,128)S(1)} %get-tuple-element.8.w_ref, f32[96,128]{1,0:T(8,128)S(1)} %get-tuple-element.9.arrived_ref, bf16[2,256,256]{2,1,0:T(8,128)(2,1)S(1)} %get-tuple-element.10.land_ref), custom_call_target="tpu_custom_call" | custom-call | tf_op jit(solution)/shard_map/pallas_call | solution.py:795

commit v7 on v6

--- a/solution.py
+++ b/solution.py
@@ -142,12 +142,29 @@
     return np.concatenate(pieces, axis=0)
 
 
-def folds():
-    heads = [(HALVES[m // 2], HALVES[m % 2]) for m in range(4)]
-    heads += [(first.T, second.T) for first, second in heads]
-    rows = np.concatenate([np.repeat(first, NPTS, axis=1) for first, _ in heads], axis=1)
-    tiles = np.concatenate([np.tile(second, (1, NPTS)) for _, second in heads], axis=1)
-    return np.concatenate([rows, tiles], axis=0).astype(np.float32)
+def places(n_dom, far, groups):
+    farp, groupp, coarsep = up(far), up(groups), up(n_dom)
+    coarse_at = 2 * farp
+    kids_at = coarse_at + 4 * coarsep
+    raw_at = kids_at + 4 * groupp
+    return farp, groupp, coarsep, coarse_at, kids_at, raw_at, raw_at + 4 * groupp
+
+
+def transforms(n_dom, far, groups):
+    farp, groupp, coarsep, coarse_at, kids_at, raw_at, used = places(n_dom, far, groups)
+    eye = np.eye(NPTS)[:, :, None]
+    first = np.repeat(eye, up(used, 128), axis=2)
+    second = first.copy()
+    for m in range(4):
+        own = slice(coarse_at + m * coarsep, coarse_at + (m + 1) * coarsep)
+        first[:, :, own] = HALVES[m // 2][:, :, None]
+        second[:, :, own] = HALVES[m % 2][:, :, None]
+        own = slice(kids_at + m * groupp, kids_at + (m + 1) * groupp)
+        first[:, :, own] = HALVES[m // 2].T[:, :, None]
+        second[:, :, own] = HALVES[m % 2].T[:, :, None]
+    rows = [first[o, i] for o in range(NPTS) for i in range(NPTS)]
+    rows += [second[b, (b + r) % NPTS] for r in range(NPTS) for b in range(NPTS)]
+    return np.stack(rows).astype(np.float32)
 
 
 def steps(
@@ -278,12 +295,14 @@
     pairs, rim, near = local_ref.shape[1], sub_ref.shape[1], near_ref.shape[1]
     far, groups = far_ref.shape[1], child_ref.shape[1]
     shifts = far // FAR
-    farp, groupp, coarsep = up(far), up(groups), up(n_dom)
-    coarse_at = 2 * farp
-    kids_at = coarse_at + coarsep
-    used = kids_at + 4 * groupp
+    farp, groupp, coarsep, coarse_at, kids_at, raw_at, used = places(n_dom, far, groups)
     sources = up(used, 128)
     lane = lax.broadcasted_iota(I32, (8, sources), 1)
+    named = lane
+    for m in range(1, 4):
+        again = (lane >= coarse_at + m * coarsep) & (lane < coarse_at + (m + 1) * coarsep)
+        named = jnp.where(again, lane - m * coarsep, named)
+    named = jnp.where(lane >= raw_at, lane - (raw_at - kids_at), named)
     row8 = lax.broadcasted_iota(I32, (8, sources), 0)
     on_low = (lane < farp) | (lane >= kids_at)
     reach = [
@@ -317,7 +336,7 @@
     def held(first, ids, base):
         total = jnp.zeros((8, sources), I32)
         for slot, value in enumerate(ids):
-            total = jnp.where(lane == first + slot, value + (1 - base * elems), total)
+            total = jnp.where(named == first + slot, value + (1 - base * elems), total)
         return total
 
     ids = held(0, [far_ref[0, c] for c in range(far)], 4)
@@ -400,23 +419,18 @@
             for c in range(1, NPTS):
                 total += reach[c] * strip(k_part, c) * deep[c]
             along_k.append(total * here)
-    fold = [
-        fold_ref[i : i + 1, :] * fold_ref[NPTS : 2 * NPTS, :] for i in range(NPTS)
-    ]
-    fold_high, fold_low = halves_of(jnp.concatenate(fold, axis=0))
     across_i = line(plane_u, DERIV)
     along_i = line([across_i[i] * plane_g[i] for i in range(NPTS)], DERIV.T)
     summed = [along_i[i] + (along_j[i] + along_k[i]) for i in range(NPTS)]
+    cross8 = [fold_ref[square + r * NPTS : square + (r + 1) * NPTS, :] for r in range(NPTS)]
+    moved = []
+    for o in range(NPTS):
+        total = fold_ref[o * NPTS : o * NPTS + 1, :] * summed[0]
+        for i in range(1, NPTS):
+            total += fold_ref[o * NPTS + i : o * NPTS + i + 1, :] * summed[i]
+        moved.append(turn(cross8, total))
+    summed = moved
     own = jnp.concatenate(summed + summed, axis=0).T
-
-    def folded(rows, first, width):
-        high, low = halves_of(rows)
-        cols = slice(first, first + width)
-        both = dot(jnp.concatenate([high, low], axis=0), fold_high[:, cols])
-        return both[0 : rows.shape[0]] + both[rows.shape[0] :] + dot(high, fold_low[:, cols])
-
-    raised = folded(own[coarse_at : coarse_at + up(coarsep, 16), 0:square], 256, 256)
-    kids = folded(own[kids_at:used, 0:square], 0, 256)
 
     half = lax.broadcasted_iota(I32, (8, 128), 1) < square
     for side in range(2):
@@ -424,17 +438,18 @@
             faces = own[side * farp + first : side * farp + first + 8]
             far_out[side, first : first + 8] = jnp.where(half, faces, pltpu.roll(faces, 6, 0))
     half_g = lax.broadcasted_iota(I32, (groupp, 128), 1) < square
-    kid = [kids[m * groupp : (m + 1) * groupp] for m in range(4)]
-    projected = jnp.where(half_g, kid[0][:, 0:128], kid[1][:, 0:128]) + jnp.where(
-        half_g, kid[2][:, 128:256], kid[3][:, 128:256]
-    )
+    kid = [own[kids_at + m * groupp : kids_at + (m + 1) * groupp] for m in range(4)]
+    projected = jnp.where(half_g, kid[0], kid[1]) + jnp.where(half_g, kid[2], kid[3])
+    half_c = lax.broadcasted_iota(I32, (coarsep, 128), 1) < square
+    raised = [own[coarse_at + m * coarsep : coarse_at + (m + 1) * coarsep] for m in range(4)]
+    raised = [jnp.where(half_c, raised[m], raised[m + 1]) for m in (0, 2)]
     peer_row = lax.broadcasted_iota(I32, (n_dom, 128), 0)
     routed = jnp.zeros((n_dom, 128), F32)
     for slot in range(groups):
         routed = jnp.where(peer_row == peer_ref[slot], projected[slot : slot + 1], routed)
     mort_out[pl.ds(0, n_dom, 8), :] = routed
-    mort_out[pl.ds(1, n_dom, 8), :] = raised[0:n_dom, 0:128]
-    mort_out[pl.ds(2, n_dom, 8), :] = raised[0:n_dom, 128:256]
+    mort_out[pl.ds(1, n_dom, 8), :] = raised[0][0:n_dom]
+    mort_out[pl.ds(2, n_dom, 8), :] = raised[1][0:n_dom]
 
     greeted = n_dom - 1 + (sub > 0).astype(I32) + (sub < n_sub - 1).astype(I32)
 
@@ -638,11 +653,10 @@
     lift = [mortar_ref[m * square : (m + 1) * square, :] for m in range(4)]
     share = []
     for m in range(4):
-        first = kids_at + m * groupp
+        first = raw_at + m * groupp
         share.append(product(joined, lift[m]) - own[first : first + groupp, 0:square])
     share = [jnp.zeros((kids_at, square), F32)] + share
-    if sources > used:
-        share.append(jnp.zeros((sources - used, square), F32))
+    share.append(jnp.zeros((sources - raw_at, square), F32))
     high, low = halves_of(jnp.concatenate(share, axis=0).T)
     add_level(0, dot(high, hot_src, over) + dot(low, hot_src, over))
     add_tiles(low_i, spread_rows(take_rows(hot1l, face1), hot0l))
@@ -751,7 +765,7 @@
         local_faces,
         sub_faces,
         near_faces,
-        jnp.asarray(folds(), F32),
+        jnp.asarray(transforms(n_dom, far_faces.shape[1], child_faces.shape[1]), F32),
         jnp.asarray(stencils(), BF16),
         jnp.asarray(mortar, F32),
     ]

time: 10.5 us -> 10.4 us (level)
  no operation moved by 1% of the time
where the time goes in v7:
time: 10.4 us; the launch traced here: 10.2 us
  Pallas kernels  10.2 us (98%)
    pallas_call x1, Pallas kernels, body(): pl.pallas_call(functools.partial(kernel, sizes, semaphores), out_shape=[p...  9.33 us
    pallas_call x1, Pallas kernels, body(): pl.pallas_call(finish, out_shape=jax.ShapeDtypeStruct((held[0] * held[1],...  0.89 us

profile of v7, /device:TPU:0, one launch (start us, length us, event | category | flops | bytes accessed | tf_op | source)
XLA Modules:
  0.0 10.2 jit_solution(17100500644930902716)
XLA Ops:
  0.0 9.3 %shard_map.127 = (f32[1024,128]{1,0:T(8,128)S(1)}, f32[96,128]{1,0:T(8,128)S(1)}, bf16[2,256,256]{2,1,0:T(8,128)(2,1)S(1)}) custom-call(f32[512,256]{1,0:T(8,128)} %refs_0_.1, f32[512,256]{1,0:T(8,128)} %refs_1_.1, s32[1,256]{1,0:T(1,128)} %bitcast.6, s32[2,64]{1,0:T(2,128)} %refs_3_.1, s32[2,32]{1,0:T(2,128)} %refs_4_.1, s32[2,32]{1,0:T(2,128)} %refs_5_.1, ...), custom_call_target="tpu_custom_call" | custom-call | tf_op jit(solution)/shard_map/pallas_call | solution.py:779
  9.3 0.9 %shard_map.128 = f32[1024,128]{1,0:T(8,128)} custom-call(f32[1024,128]{1,0:T(8,128)S(1)} %get-tuple-element.8.w_ref, f32[96,128]{1,0:T(8,128)S(1)} %get-tuple-element.9.arrived_ref, bf16[2,256,256]{2,1,0:T(8,128)(2,1)S(1)} %get-tuple-element.10.land_ref), custom_call_target="tpu_custom_call" | custom-call | tf_op jit(solution)/shard_map/pallas_call | solution.py:809

commit v8 on v7

--- a/solution.py
+++ b/solution.py
@@ -482,9 +482,33 @@
     def far_there(side, s):
         return me >= s + 2 if side == 0 else me + s + 2 < n_dom
 
+    sides = [
+        (sub > 0, 0, 1, (me, sub - 1)),
+        (sub < n_sub - 1, 1, 0, (me, sub + 1)),
+        (me > 0, 2, 3, (me - 1, sub)),
+        (me < n_dom - 1, 3, 2, (me + 1, sub)),
+    ]
+
+    def side_copy(mine, theirs, device):
+        return pltpu.make_async_remote_copy(
+            src_ref=side_out.at[mine],
+            dst_ref=side_in.at[theirs],
+            send_sem=side_send.at[mine],
+            recv_sem=side_recv.at[theirs],
+            device_id=device,
+            device_id_type=MESH,
+        )
+
+    def send_sides():
+        for there, mine, theirs, device in sides:
+            @pl.when(there)
+            def _():
+                side_copy(mine, theirs, device).start()
+
+    def meet():
+        pl.semaphore_wait(barrier, greeted)
+
     def send_messages():
-        pl.semaphore_wait(barrier, greeted)
-
         def start_all(step, carry):
             mail(step, False).start()
             return carry
@@ -500,6 +524,7 @@
 
     @pl.when(jnp.logical_not(early))
     def _():
+        meet()
         send_messages()
 
     for copy in small[6:]:
@@ -507,10 +532,11 @@
 
     hot0l = hot_rows([column(local_ref[1:2], up(pairs))], 0, elems)
     hot1l = hot_rows([column(local_ref[0:1], up(pairs))], elems, elems)
-    hot0s = hot_rows([column(sub_ref[0:1], up(rim))], 0, elems)
-    hot1s = hot_rows([column(sub_ref[1:2], up(rim))], elems, elems)
-    hot2 = hot_rows([column(near_ref[0:1], up(near))], 2 * elems, elems)
-    hot3 = hot_rows([column(near_ref[1:2], up(near))], 3 * elems, elems)
+    folded = side_out.shape[1]
+    hot0s = hot_rows([column(sub_ref[0:1], 2 * folded)], 0, elems)
+    hot1s = hot_rows([column(sub_ref[1:2], 2 * folded)], elems, elems)
+    hot2 = hot_rows([column(near_ref[0:1], 2 * folded)], 2 * elems, elems)
+    hot3 = hot_rows([column(near_ref[1:2], 2 * folded)], 3 * elems, elems)
 
     sub8 = lax.broadcasted_iota(I32, (8, elems), 0)
     weight = jnp.zeros((8, elems), F32)
@@ -589,36 +615,20 @@
     low_i, high_i = ([(i, j) for j in range(NPTS)] for i in (0, last))
     low_j, high_j = ([(i, j) for i in range(NPTS)] for j in (0, last))
     face0, face1, face2, face3 = (face_of(tiles) for tiles in (low_i, high_i, low_j, high_j))
-    side_out[0, 0:rim, 0:square] = take_rows(hot0s, face0)[0:rim]
-    side_out[1, 0:rim, 0:square] = take_rows(hot1s, face1)[0:rim]
-    side_out[2, 0:near, 0:square] = take_rows(hot2, face2)[0:near]
-    side_out[3, 0:near, 0:square] = take_rows(hot3, face3)[0:near]
+    faces = ((hot0s, face0), (hot1s, face1), (hot2, face2), (hot3, face3))
+    for slot, (spots, face) in enumerate(faces):
+        taken = take_rows(spots, face)
+        side_out[slot] = jnp.concatenate([taken[0:folded], taken[folded:]], axis=1)
 
     @pl.when(early)
     def _():
+        meet()
+        send_sides()
         send_messages()
 
-    sides = [
-        (sub > 0, 0, 1, (me, sub - 1)),
-        (sub < n_sub - 1, 1, 0, (me, sub + 1)),
-        (me > 0, 2, 3, (me - 1, sub)),
-        (me < n_dom - 1, 3, 2, (me + 1, sub)),
-    ]
-
-    def side_copy(mine, theirs, device):
-        return pltpu.make_async_remote_copy(
-            src_ref=side_out.at[mine],
-            dst_ref=side_in.at[theirs],
-            send_sem=side_send.at[mine],
-            recv_sem=side_recv.at[theirs],
-            device_id=device,
-            device_id_type=MESH,
-        )
-
-    for there, mine, theirs, device in sides:
-        @pl.when(there)
-        def _():
-            side_copy(mine, theirs, device).start()
+    @pl.when(jnp.logical_not(early))
+    def _():
+        send_sides()
 
     keyed = up(2 * farp + 8 * n_dom, 128)
 
@@ -662,17 +672,22 @@
     add_tiles(low_i, spread_rows(take_rows(hot1l, face1), hot0l))
     add_tiles(high_i, spread_rows(take_rows(hot0l, face0), hot1l))
 
-    for there, mine, theirs, device in sides:
-        @pl.when(there)
-        def _():
-            side_copy(mine, mine, device).wait()
-
-    add_tiles(low_i, spread_rows(side_in[0, 0:rim, 0:square], hot0s))
-    add_tiles(high_i, spread_rows(side_in[1, 0:rim, 0:square], hot1s))
-    add2 = spread_rows(side_in[2, 0:near, 0:square], hot2)
-    add3 = spread_rows(side_in[3, 0:near, 0:square], hot3)
-    add_tiles(low_j, add2)
-    add_tiles(high_j, add3)
+    targets = ((hot0s, low_i), (hot1s, high_i), (hot2, low_j), (hot3, high_j))
+    for group in ((0, 2, 3), (1,)):
+        for slot in group:
+            there, mine, _, device = sides[slot]
+
+            @pl.when(there)
+            def _():
+                side_copy(mine, mine, device).wait()
+
+        for slot in group:
+            spots, tiles = targets[slot]
+            both = side_in[slot].T
+            pieces = [both[0:square], both[square:]]
+            rows = [jnp.concatenate(halves_of(piece), axis=0) for piece in pieces]
+            added = dot(rows[0], spots[0:folded]) + dot(rows[1], spots[folded:])
+            add_tiles(tiles, added[0:square] + added[square:])
 
     def sent_all(step, carry):
         mail(step, True).wait_send()
@@ -759,7 +774,7 @@
     mortar = np.concatenate([m.T for m in krons], axis=0)
     far_rows = up(far_faces.shape[1])
     held = (elems // 128, NPTS**3, 128)
-    side_rows = up(max(sub_faces.shape[1], near_faces.shape[1]))
+    side_rows = up(max(sub_faces.shape[1], near_faces.shape[1]), 32) // 2
     small = [
         levels.reshape(1, elems),
         local_faces,

time: 10.4 us -> 10.4 us (level)
  no operation moved by 1% of the time
where the time goes in v8:
time: 10.4 us; the launch traced here: 10.2 us
  Pallas kernels  10.2 us (98%)
    pallas_call x1, Pallas kernels, body(): pl.pallas_call(functools.partial(kernel, sizes, semaphores), out_shape=[p...  9.33 us
    pallas_call x1, Pallas kernels, body(): pl.pallas_call(finish, out_shape=jax.ShapeDtypeStruct((held[0] * held[1],...  0.89 us

profile of v8, /device:TPU:0, one launch (start us, length us, event | category | flops | bytes accessed | tf_op | source)
XLA Modules:
  0.0 10.2 jit_solution(6940994773060129471)
XLA Ops:
  0.0 9.3 %shard_map.127 = (f32[1024,128]{1,0:T(8,128)S(1)}, f32[96,128]{1,0:T(8,128)S(1)}, bf16[2,256,256]{2,1,0:T(8,128)(2,1)S(1)}) custom-call(f32[512,256]{1,0:T(8,128)} %refs_0_.1, f32[512,256]{1,0:T(8,128)} %refs_1_.1, s32[1,256]{1,0:T(1,128)} %bitcast.6, s32[2,64]{1,0:T(2,128)} %refs_3_.1, s32[2,32]{1,0:T(2,128)} %refs_4_.1, s32[2,32]{1,0:T(2,128)} %refs_5_.1, ...), custom_call_target="tpu_custom_call" | custom-call | tf_op jit(solution)/shard_map/pallas_call | solution.py:794
  9.3 0.9 %shard_map.128 = f32[1024,128]{1,0:T(8,128)} custom-call(f32[1024,128]{1,0:T(8,128)S(1)} %get-tuple-element.8.w_ref, f32[96,128]{1,0:T(8,128)S(1)} %get-tuple-element.9.arrived_ref, bf16[2,256,256]{2,1,0:T(8,128)(2,1)S(1)} %get-tuple-element.10.land_ref), custom_call_target="tpu_custom_call" | custom-call | tf_op jit(solution)/shard_map/pallas_call | solution.py:824
